TPU v7x, 32 devices: a whole 2x2x4 slice. The times are simulated.
32 devices in a mesh: seq: 8 (over z, y), ch: 4 (over x, core).
Axes of the slice: x: 2, y: 2, z: 4, core: 2. Of those that a mesh axis runs over, the one named last changes fastest.
Arguments:
- query_input: bfloat16 [1024, 2048], P('seq', 'ch'), may hold values from -6 to 6
- key_input: bfloat16 [1024, 2048], P('seq', 'ch'), may hold values from -6 to 6
- value_input: bfloat16 [1024, 2048], P('seq', 'ch'), may hold values from -6 to 6
- cotangent: bfloat16 [1024, 2048], P('seq', 'ch'), may hold values from -6 to 6
- filter_taps: float32 [1024, 2048], P('seq', 'ch'), may hold values from -0.1875 to 0.1875
- skip_gain: float32 [2048], P('ch'), may hold values from -2 to 2
Outputs:
- output: bfloat16 [1024, 2048], P('seq', 'ch')
- query_grad: bfloat16 [1024, 2048], P('seq', 'ch')
- key_grad: bfloat16 [1024, 2048], P('seq', 'ch')
- value_grad: bfloat16 [1024, 2048], P('seq', 'ch')
- filter_grad: float32 [1024, 2048], P('seq', 'ch')
- skip_grad: float32 [2048], P('ch')
- grad_rms: float32 [], replicated
All inputs are finite; a program needn't handle non-finite values.
Results may differ from a plain program's by a relative error of at most 0.0014.
Values sent between devices are 32-bit elements; how exact they have to be, the bound alone decides.
A program may use at most 64 MiB of HBM per device.

v0:
```python
import functools
import math

import jax
import jax.numpy as jnp
import numpy as np
from jax import lax
from jax.experimental import pallas as pl
from jax.experimental.pallas import tpu as pltpu
from jax.sharding import PartitionSpec as P

LANES = 128
MESH = pl.DeviceIdType.MESH


def complex_mul(left_op, right_op):
    return jnp.stack(
        [
            left_op[0] * right_op[0] - left_op[1] * right_op[1],
            left_op[0] * right_op[1] + left_op[1] * right_op[0],
        ]
    )


def conj_of(stacked):
    return jnp.stack([stacked[0], -stacked[1]])


def dft_table(length, direction):
    counter = jnp.arange(length)
    angles = (
        2.0 * math.pi / length * (counter[:, None] * counter[None, :] % length).astype(jnp.float32)
    )
    return (jnp.cos(angles), direction * jnp.sin(angles))


def dft_along(stacked, length, direction, pattern):
    table_re, table_im = dft_table(length, direction)

    def contract(table, part_in):
        return jnp.einsum(pattern, table, part_in, precision=lax.Precision.HIGHEST)

    real_out = contract(table_re, stacked[0]) - contract(table_im, stacked[1])
    imag_out = contract(table_re, stacked[1]) + contract(table_im, stacked[0])
    return jnp.stack([real_out, imag_out])


def grid_twiddle(devices, block, direction):
    seq_length = devices * block
    counter = jnp.arange(devices)[:, None] * jnp.arange(block)[None, :] % seq_length
    angles = direction * 2.0 * math.pi / seq_length * counter.astype(jnp.float32)
    return jnp.stack([jnp.cos(angles), jnp.sin(angles)])[:, None, None]


def local_forward(stacked, devices, block):
    array_shape = stacked.shape
    stacked = stacked.reshape(array_shape[0], array_shape[1], array_shape[2], devices, block)
    stacked = dft_along(stacked, devices, -1.0, "kj,scjp->sckp")
    stacked = complex_mul(stacked, grid_twiddle(devices, block, -1.0))
    return dft_along(stacked, block, -1.0, "kp,scjp->scjk")


def local_inverse(stacked, devices, block):
    stacked = dft_along(stacked, block, 1.0, "kp,scjp->scjk")
    stacked = complex_mul(stacked, grid_twiddle(devices, block, 1.0))
    stacked = dft_along(stacked, devices, 1.0, "kj,scjp->sckp")
    array_shape = stacked.shape
    return stacked.reshape(array_shape[0], array_shape[1], array_shape[2], devices * block) / (
        devices * block
    )


def modulated(signals, cosine, sine_part):
    zero_part = jnp.zeros_like(signals)
    return jnp.stack(
        [
            jnp.concatenate([signals, signals * cosine]),
            jnp.concatenate([zero_part, -signals * sine_part]),
        ]
    )


def spectral_products(spectrum):
    mixed_spec = spectrum[:, 0::3]
    gated_spec = spectrum[:, 1::3]
    taps_spec = spectrum[:, 2::3]
    out_spec = complex_mul(mixed_spec, taps_spec)
    back_spec = complex_mul(gated_spec, conj_of(taps_spec))
    grad_spec = complex_mul(gated_spec, conj_of(mixed_spec))
    return jnp.stack(
        [
            out_spec[:, 0],
            back_spec[:, 0],
            grad_spec[:, 0],
            out_spec[:, 1],
            back_spec[:, 1],
            grad_spec[:, 1],
        ],
        axis=1,
    )


def unfold(series, cosine, sine_part):
    return tuple(
        (
            0.5
            * (
                series[0, signal_index]
                + cosine * series[0, signal_index + 3]
                - sine_part * series[1, signal_index + 3]
            )
            for signal_index in range(3)
        )
    )


def channel_local(mixed_in, gated_cot, filter_taps, devices):
    pieces = (
        lax.all_to_all(mixed_in, "seq", split_axis=1, concat_axis=0, tiled=True),
        lax.all_to_all(gated_cot, "seq", split_axis=1, concat_axis=0, tiled=True),
        lax.all_to_all(filter_taps, "seq", split_axis=1, concat_axis=0, tiled=True),
    )
    laid = jnp.transpose(jnp.stack(pieces), (0, 2, 1))
    seq_length = laid.shape[2]
    block = seq_length // devices
    angles = math.pi / seq_length * jnp.arange(seq_length).astype(jnp.float32)
    cosine = jnp.cos(angles)
    sine_row = jnp.sin(angles)
    spectrum = local_forward(modulated(laid, cosine, sine_row), devices, block)
    series = local_inverse(spectral_products(spectrum), devices, block)
    results = unfold(series, cosine, sine_row)
    return (
        lax.all_to_all(results[0].T, "seq", split_axis=0, concat_axis=1, tiled=True),
        lax.all_to_all(results[1].T, "seq", split_axis=0, concat_axis=1, tiled=True),
        lax.all_to_all(results[2].T, "seq", split_axis=0, concat_axis=1, tiled=True),
    )


def body(query_input, key_input, value_input, cotangent, filter_taps, skip_gain):
    devices = lax.axis_size("seq")
    row_count, channels = query_input.shape
    seq_length = row_count * devices
    query_val = query_input.astype(jnp.float32)
    key_val = key_input.astype(jnp.float32)
    value_val = value_input.astype(jnp.float32)
    cot_val = cotangent.astype(jnp.float32)
    mixed_in = key_val * value_val
    gated_cot = query_val * cot_val
    conv_out, back_conv, kernel_grad = channel_local(mixed_in, gated_cot, filter_taps, devices)
    inner_sum = conv_out + skip_gain[None, :] * mixed_in
    mixed_grad = back_conv + skip_gain[None, :] * gated_cot
    output = (query_val * inner_sum).astype(jnp.bfloat16)
    query_grad = (cot_val * inner_sum).astype(jnp.bfloat16)
    key_grad = (mixed_grad * value_val).astype(jnp.bfloat16)
    value_grad = (mixed_grad * key_val).astype(jnp.bfloat16)
    time_scale = 1.0 / math.sqrt(seq_length)
    filter_grad = kernel_grad * time_scale
    filter_sq = jnp.sum(filter_grad * filter_grad)
    skip_part = jnp.sum(gated_cot * mixed_in, axis=0) * time_scale
    skip_grad = lax.psum(skip_part, "seq")
    total_sq = lax.psum(filter_sq + jnp.sum(skip_grad * skip_grad) / devices, ("seq", "ch"))
    grad_rms = jnp.sqrt(total_sq / (channels * lax.axis_size("ch") * (seq_length + 1)))
    return (output, query_grad, key_grad, value_grad, filter_grad, skip_grad, grad_rms)


def split_high_low(array):
    high = array.astype(jnp.bfloat16)
    return high, (array - high.astype(jnp.float32)).astype(jnp.bfloat16)


def half_tables(points):
    odd = 2 * np.arange(points, dtype=np.int64) + 1
    angles = math.pi / (4 * points) * (odd[:, None] * odd[None, :] % (8 * points))
    parts = []
    for table in (np.cos(angles), np.sin(angles)):
        table = table.astype(np.float32)
        high = table.astype(jnp.bfloat16)
        parts += [high, (table - high.astype(np.float32)).astype(jnp.bfloat16)]
    shift = math.pi / (4 * points) * odd[:, None] * np.ones((1, LANES))
    return np.stack(parts), np.stack([np.cos(shift), np.sin(shift)]).astype(np.float32)


def kernel(
    devices, groups, count,
    q_ref, k_ref, v_ref, c_ref, h_ref, table_hbm, twist_hbm,
    flat, dskip_ref, rms_ref,
    x_buf, g_buf, wide, send, recv, spec, prod, back, home, tail, tail_home, sq_send, sq_recv,
    table, twist, send_sem, recv_sem, own_sem, tail_send, tail_recv, sq_ssem, sq_rsem, load_sem,
):
    me = lax.axis_index("seq")
    mine = lax.axis_index("ch")
    rows, channels = q_ref.shape
    half = rows // 2
    points = half * devices
    low = LANES // 2
    time_scale = 1.0 / math.sqrt(2 * points)

    barrier = pltpu.get_barrier_semaphore()
    for k in range(1, devices):
        pl.semaphore_signal(
            barrier, inc=1, device_id={"seq": lax.rem(me + k, devices)}, device_id_type=MESH
        )
    for k in range(1, groups):
        pl.semaphore_signal(
            barrier, inc=1, device_id={"ch": lax.rem(mine + k, groups)}, device_id_type=MESH
        )
    loads = (
        pltpu.make_async_copy(table_hbm, table, load_sem.at[0]),
        pltpu.make_async_copy(twist_hbm, twist, load_sem.at[1]),
    )
    for load in loads:
        load.start()

    def remote(source, target, slot, k):
        peer = lax.rem(me + k, devices)
        return pltpu.make_async_remote_copy(
            src_ref=source.at[peer],
            dst_ref=target.at[me],
            send_sem=send_sem.at[slot, k],
            recv_sem=recv_sem.at[slot, k],
            device_id={"seq": peer},
            device_id_type=MESH,
        )

    def own(source, target, slot):
        return pltpu.make_async_copy(source.at[me], target.at[me], own_sem.at[slot])

    def tail_copy(k):
        peer = lax.rem(me + k, devices)
        return pltpu.make_async_remote_copy(
            src_ref=tail,
            dst_ref=tail_home.at[me],
            send_sem=tail_send.at[k],
            recv_sem=tail_recv.at[k],
            device_id={"seq": peer},
            device_id_type=MESH,
        )

    def square_copy(k):
        peer = lax.rem(mine + k, groups)
        return pltpu.make_async_remote_copy(
            src_ref=sq_send,
            dst_ref=sq_recv.at[mine],
            send_sem=sq_ssem.at[k],
            recv_sem=sq_rsem.at[k],
            device_id={"ch": peer},
            device_id_type=MESH,
        )

    def start_all(source, target, slot):
        for k in range(1, devices):
            remote(source, target, slot, k).start()
        own(source, target, slot).start()

    def wait_arrivals(source, target, slot):
        for k in range(1, devices):
            remote(source, target, slot, k).wait_recv()
        own(source, target, slot).wait()

    first = lax.broadcasted_iota(jnp.int32, (half, LANES), 1) < low

    def pack(source, signal):
        for j in range(channels // LANES):
            even = source[j, pl.ds(0, half, stride=2), :]
            odd = source[j, pl.ds(1, half, stride=2), :]
            send[signal, 2 * j] = jnp.where(first, even, pltpu.roll(odd, low, 1))
            send[signal, 2 * j + 1] = jnp.where(first, pltpu.roll(even, low, 1), odd)

    def unpack(signal):
        for j in range(channels // LANES):
            left = home[signal, 2 * j]
            right = home[signal, 2 * j + 1]
            flat[signal, j, pl.ds(0, half, stride=2), :] = jnp.where(
                first, left, pltpu.roll(right, low, 1)
            )
            flat[signal, j, pl.ds(1, half, stride=2), :] = jnp.where(
                first, pltpu.roll(left, low, 1), right
            )

    def columns_of(j):
        return pl.ds(j * LANES, LANES)

    blocks = channels // LANES
    for j in range(blocks):
        at = columns_of(j)
        x_buf[j] = k_ref[:, at].astype(jnp.float32) * v_ref[:, at].astype(jnp.float32)
    pack(x_buf, 0)
    pl.semaphore_wait(barrier, devices + groups - 2)
    start_all(send.at[0], recv.at[0], 0)
    for j in range(blocks):
        at = columns_of(j)
        g_buf[j] = q_ref[:, at].astype(jnp.float32) * c_ref[:, at].astype(jnp.float32)
    pack(g_buf, 1)
    start_all(send.at[1], recv.at[1], 1)
    for j in range(blocks):
        wide[j] = h_ref[:, columns_of(j)]
    pack(wide, 2)
    start_all(send.at[2], recv.at[2], 2)
    for load in loads:
        load.wait()

    def times(which, high, rest):
        both = jnp.concatenate([high, rest], axis=1)
        main = jnp.dot(table[2 * which], both, preferred_element_type=jnp.float32)
        small = jnp.dot(table[2 * which + 1], high, preferred_element_type=jnp.float32)
        return main[:, :LANES] + (main[:, LANES:] + small)

    def forward(signal):
        high, rest = split_high_low(recv[signal].reshape(points, LANES))
        spec[signal, 0] = times(0, high, rest)
        spec[signal, 1] = -times(1, high, rest)

    def inverse(slot, scale):
        real_high, real_rest = split_high_low(prod[0])
        imag_high, imag_rest = split_high_low(prod[1])
        series = times(0, real_high, real_rest) - times(1, imag_high, imag_rest)
        series = series * (scale / points)
        back[slot] = series.reshape(devices, half, LANES)
        return series

    step = 32

    def halves(ref_row, part, at):
        value = spec[ref_row, part, at, :]
        turned = pltpu.roll(value, low, 1)
        left = lax.broadcasted_iota(jnp.int32, (step, LANES), 1) < low
        return value, turned, jnp.where(left, value, turned), jnp.where(left, turned, value)

    def products(signal, other, conjugate):
        sign = jnp.where(lax.broadcasted_iota(jnp.int32, (step, LANES), 1) < low, 1.0, -1.0)

        @pl.loop(0, points // step)
        def _(index):
            at = pl.ds(pl.multiple_of(index * step, step), step)
            cosine = twist[0, at, :]
            sine = twist[1, at, :]
            signed = sine * sign
            _, _, even_re, odd_re = halves(other, 0, at)
            _, _, even_im, odd_im = halves(other, 1, at)
            a_re, as_re, _, _ = halves(signal, 0, at)
            a_im, as_im, _, _ = halves(signal, 1, at)
            p_re = even_re * cosine - even_im * sine
            p_im = even_im * cosine + even_re * sine
            if conjugate:
                r_re = odd_re * cosine - odd_im * signed
                r_im = odd_im * cosine + odd_re * signed
                prod[0, at, :] = a_re * p_re + a_im * p_im + (as_re * r_re + as_im * r_im)
                prod[1, at, :] = a_im * p_re - a_re * p_im + (as_im * r_re - as_re * r_im)
            else:
                r_re = odd_re * cosine + odd_im * signed
                r_im = odd_im * cosine - odd_re * signed
                prod[0, at, :] = a_re * p_re - a_im * p_im + (as_re * r_re - as_im * r_im)
                prod[1, at, :] = a_im * p_re + a_re * p_im + (as_im * r_re + as_re * r_im)

    wait_arrivals(send.at[0], recv.at[0], 0)
    forward(0)
    wait_arrivals(send.at[1], recv.at[1], 1)
    forward(1)
    products(1, 0, True)
    series = inverse(0, time_scale)
    start_all(back.at[0], home.at[0], 3)
    direct = jnp.sum(
        (recv[0] * recv[1]).reshape(points // 8, 8, LANES), axis=0
    )
    direct = jnp.sum(direct, axis=0, keepdims=True)
    direct = jnp.broadcast_to(direct, (8, LANES)) * time_scale
    direct = direct + pltpu.roll(direct, low, 1)
    squares = jnp.sum((series * series).reshape(points // 8, 8, LANES), axis=0)
    squares = squares + direct * direct * (1.0 / 16.0)
    sq_send[...] = squares
    for k in range(1, groups):
        square_copy(k).start()
    sq_own = pltpu.make_async_copy(sq_send, sq_recv.at[mine], load_sem.at[2])
    sq_own.start()

    wait_arrivals(send.at[2], recv.at[2], 2)
    forward(2)
    products(0, 2, False)
    inverse(1, 1.0)
    start_all(back.at[1], home.at[1], 4)
    for k in range(1, groups):
        square_copy(k).wait_recv()
    sq_own.wait()
    total = sq_recv[0]
    for k in range(1, groups):
        total = total + sq_recv[k]
    tail[0] = direct
    tail[1] = total
    for k in range(1, devices):
        tail_copy(k).start()
    tail_own = pltpu.make_async_copy(tail, tail_home.at[me], load_sem.at[3])
    tail_own.start()
    products(1, 2, True)
    inverse(2, 1.0)
    start_all(back.at[2], home.at[2], 5)

    wait_arrivals(back.at[0], home.at[0], 3)
    unpack(0)

    wait_arrivals(back.at[1], home.at[1], 4)
    unpack(1)

    for k in range(1, devices):
        tail_copy(k).wait_recv()
    tail_own.wait()
    total = tail_home[0, 1]
    for k in range(1, devices):
        total = total + tail_home[k, 1]
    total = jnp.sum(jnp.sum(total, axis=0, keepdims=True), axis=1, keepdims=True)
    rms_ref[...] = total / count
    for j in range(blocks):
        left = lax.broadcasted_iota(jnp.int32, (8, LANES), 1) < low
        both = jnp.where(left, tail_home[2 * j, 0], tail_home[2 * j + 1, 0])
        dskip_ref[:, columns_of(j)] = both[0:1]

    wait_arrivals(back.at[2], home.at[2], 5)
    unpack(2)

    for k in range(1, devices):
        for slot in range(3):
            remote(send.at[slot], recv.at[slot], slot, k).wait_send()
            remote(back.at[slot], home.at[slot], slot + 3, k).wait_send()
        tail_copy(k).wait_send()
    for k in range(1, groups):
        square_copy(k).wait_send()


def gate(
    q_ref, k_ref, v_ref, c_ref, skip_ref, flat, direct_ref, mean_ref,
    out_ref, dq_ref, dk_ref, dv_ref, dh_ref, dskip_ref, rms_ref,
):
    query_val = q_ref[...].astype(jnp.float32)
    key_val = k_ref[...].astype(jnp.float32)
    value_val = v_ref[...].astype(jnp.float32)
    cot_val = c_ref[...].astype(jnp.float32)
    skip = skip_ref[...]
    inner = flat[1, 0] + skip * (key_val * value_val)
    grad = flat[2, 0] + skip * (query_val * cot_val)
    out_ref[...] = (query_val * inner).astype(jnp.bfloat16)
    dq_ref[...] = (cot_val * inner).astype(jnp.bfloat16)
    dk_ref[...] = (grad * value_val).astype(jnp.bfloat16)
    dv_ref[...] = (grad * key_val).astype(jnp.bfloat16)
    dh_ref[...] = flat[0, 0]
    dskip_ref[...] = direct_ref[...]
    rms_ref[...] = jnp.sqrt(mean_ref[...])


def fused_body(query_input, key_input, value_input, cotangent, filter_taps, skip_gain):
    devices = lax.axis_size("seq")
    groups = lax.axis_size("ch")
    rows, channels = query_input.shape
    half = rows // 2
    points = half * devices
    tables, twists = half_tables(points)
    count = float(channels * groups * (rows * devices + 1))
    vmem = pl.BlockSpec(memory_space=pltpu.VMEM)
    hbm = pl.BlockSpec(memory_space=pl.ANY)
    narrow = jax.ShapeDtypeStruct((rows, channels), jnp.bfloat16)
    moved = (3, devices, half, LANES)
    blocks = channels // LANES
    flat, direct, rms = pl.pallas_call(
        functools.partial(kernel, devices, groups, count),
        out_shape=(
            jax.ShapeDtypeStruct((3, blocks, rows, LANES), jnp.float32),
            jax.ShapeDtypeStruct((1, channels), jnp.float32),
            jax.ShapeDtypeStruct((1, 1), jnp.float32),
        ),
        in_specs=[vmem] * 5 + [hbm] * 2,
        out_specs=(vmem,) * 3,
        scratch_shapes=[
            pltpu.VMEM((channels // LANES, rows, LANES), jnp.float32),
            pltpu.VMEM((channels // LANES, rows, LANES), jnp.float32),
            pltpu.VMEM((channels // LANES, rows, LANES), jnp.float32),
            pltpu.VMEM(moved, jnp.float32),
            pltpu.VMEM(moved, jnp.float32),
            pltpu.VMEM((3, 2, points, LANES), jnp.float32),
            pltpu.VMEM((2, points, LANES), jnp.float32),
            pltpu.VMEM(moved, jnp.float32),
            pltpu.VMEM(moved, jnp.float32),
            pltpu.VMEM((2, 8, LANES), jnp.float32),
            pltpu.VMEM((devices, 2, 8, LANES), jnp.float32),
            pltpu.VMEM((8, LANES), jnp.float32),
            pltpu.VMEM((groups, 8, LANES), jnp.float32),
            pltpu.VMEM(tables.shape, jnp.bfloat16),
            pltpu.VMEM(twists.shape, jnp.float32),
            pltpu.SemaphoreType.DMA((6, devices)),
            pltpu.SemaphoreType.DMA((6, devices)),
            pltpu.SemaphoreType.DMA((6,)),
            pltpu.SemaphoreType.DMA((devices,)),
            pltpu.SemaphoreType.DMA((devices,)),
            pltpu.SemaphoreType.DMA((groups,)),
            pltpu.SemaphoreType.DMA((groups,)),
            pltpu.SemaphoreType.DMA((4,)),
        ],
        compiler_params=pltpu.CompilerParams(collective_id=0, has_side_effects=True),
    )(
        query_input, key_input, value_input, cotangent, filter_taps, jnp.asarray(tables), jnp.asarray(twists),
    )
    column = pl.BlockSpec((rows, LANES), lambda j: (0, j))
    line = pl.BlockSpec((1, LANES), lambda j: (0, j))
    single = pl.BlockSpec((1, 1), lambda j: (0, 0))
    results = pl.pallas_call(
        gate,
        grid=(blocks,),
        out_shape=(
            narrow,
            narrow,
            narrow,
            narrow,
            jax.ShapeDtypeStruct((rows, channels), jnp.float32),
            jax.ShapeDtypeStruct((1, channels), jnp.float32),
            jax.ShapeDtypeStruct((1, 1), jnp.float32),
        ),
        in_specs=[column] * 4
        + [line, pl.BlockSpec((3, 1, rows, LANES), lambda j: (0, j, 0, 0)), line, single],
        out_specs=[column] * 5 + [line, single],
    )(
        query_input, key_input, value_input, cotangent,
        skip_gain.reshape(1, channels), flat, direct, rms,
    )
    return (*results[:5], results[5].reshape(channels), results[6].reshape(()))


def pick_body(query_input, *others):
    devices = lax.axis_size("seq")
    rows, channels = query_input.shape
    fits = 2 * channels == LANES * devices and channels % LANES == 0 and rows % 16 == 0
    chosen = fused_body if fits and rows * devices <= 2048 else body
    return chosen(query_input, *others)


def solution(mesh):
    return jax.shard_map(
        pick_body,
        mesh=mesh,
        in_specs=(
            P("seq", "ch"),
            P("seq", "ch"),
            P("seq", "ch"),
            P("seq", "ch"),
            P("seq", "ch"),
            P("ch"),
        ),
        out_specs=(
            P("seq", "ch"),
            P("seq", "ch"),
            P("seq", "ch"),
            P("seq", "ch"),
            P("seq", "ch"),
            P("ch"),
            P(),
        ),
        check_vma=False,
    )
```

profile of v0, /device:TPU:0, one launch (start us, length us, event | category | flops | bytes accessed | tf_op | source)
XLA Modules:
  0.0 50.4 jit_solution(13042687928183093623)
XLA Ops:
  0.6 45.7 %shard_map.135 = (f32[3,4,128,128]{3,2,1,0:T(8,128)}, f32[1,512]{1,0:T(1,128)}, f32[1,1]{1,0:T(1,128)}) custom-call(bf16[128,512]{1,0:T(8,128)(2,1)} %q_ref.3, bf16[128,512]{1,0:T(8,128)(2,1)} %k_ref.3, bf16[128,512]{1,0:T(8,128)(2,1)} %v_ref.3, bf16[128,512]{1,0:T(8,128)(2,1)} %c_ref.3, f32[128,512]{1,0:T(8,128)} %h_ref.1, ...), custom_call_target="tpu_custom_call" | custom-call | tf_op jit(solution)/shard_map/pallas_call | solution.py:461
  46.3 4.1 %shard_map.136 = (bf16[128,512]{1,0:T(8,128)(2,1)}, bf16[128,512]{1,0:T(8,128)(2,1)}, bf16[128,512]{1,0:T(8,128)(2,1)}, bf16[128,512]{1,0:T(8,128)(2,1)}, f32[12...) custom-call(bf16[128,512]{1,0:T(8,128)(2,1)} %q_ref.3, bf16[128,512]{1,0:T(8,128)(2,1)} %k_ref.3, ...), custom_call_target="tpu_custom_call" | custom-call | tf_op jit(solution)/shard_map/pallas_call | solution.py:502
where the time goes:
time: 50.6 us; the launch traced here: 50.4 us
  Pallas kernels  49.8 us (98%)
  between operations  0.64 us (1%)
    pallas_call x1, Pallas kernels, fused_body(): pl.pallas_call(functools.partial(kernel, devices, groups, count), out_sha...  45.7 us
    pallas_call x1, Pallas kernels, fused_body(): pl.pallas_call(gate, grid=(blocks,), out_shape=(narrow, narrow, narrow, n...  4.13 us

commit v1 on v0

--- a/solution.py
+++ b/solution.py
@@ -182,14 +182,14 @@
 
 def kernel(
     devices, groups, count,
-    q_ref, k_ref, v_ref, c_ref, h_ref, table_hbm, twist_hbm,
-    flat, dskip_ref, rms_ref,
-    x_buf, g_buf, wide, send, recv, spec, prod, back, home, tail, tail_home, sq_send, sq_recv,
-    table, twist, send_sem, recv_sem, own_sem, tail_send, tail_recv, sq_ssem, sq_rsem, load_sem,
+    q_hbm, k_hbm, v_hbm, c_hbm, h_hbm, skip_hbm, table_hbm, twist_hbm,
+    out_ref, dq_ref, dk_ref, dv_ref, dh_ref, dskip_ref, rms_ref,
+    q_ref, k_ref, v_ref, c_ref, skip_ref, x_buf, g_buf, wide, flat, send, recv, spec, prod, back, home, tail, tail_home, sq_send, sq_recv,
+    table, twist, send_sem, recv_sem, own_sem, tail_send, tail_recv, sq_ssem, sq_rsem, load_sem, in_sem,
 ):
     me = lax.axis_index("seq")
     mine = lax.axis_index("ch")
-    rows, channels = q_ref.shape
+    rows, channels = q_hbm.shape
     half = rows // 2
     points = half * devices
     low = LANES // 2
@@ -204,6 +204,20 @@
         pl.semaphore_signal(
             barrier, inc=1, device_id={"ch": lax.rem(mine + k, groups)}, device_id_type=MESH
         )
+    blocks = channels // LANES
+
+    def columns_of(j):
+        return pl.ds(j * LANES, LANES)
+
+    inputs = tuple(
+        pltpu.make_async_copy(source, target, in_sem.at[index])
+        for index, (source, target) in enumerate(
+            [(k_hbm, k_ref), (v_hbm, v_ref), (q_hbm, q_ref), (c_hbm, c_ref), (skip_hbm, skip_ref)]
+            + [(h_hbm.at[:, columns_of(j)], wide.at[j]) for j in range(blocks)]
+        )
+    )
+    for load in inputs:
+        load.start()
     loads = (
         pltpu.make_async_copy(table_hbm, table, load_sem.at[0]),
         pltpu.make_async_copy(twist_hbm, twist, load_sem.at[1]),
@@ -277,23 +291,23 @@
                 first, pltpu.roll(left, low, 1), right
             )
 
-    def columns_of(j):
-        return pl.ds(j * LANES, LANES)
-
-    blocks = channels // LANES
+    inputs[0].wait()
+    inputs[1].wait()
     for j in range(blocks):
         at = columns_of(j)
         x_buf[j] = k_ref[:, at].astype(jnp.float32) * v_ref[:, at].astype(jnp.float32)
     pack(x_buf, 0)
     pl.semaphore_wait(barrier, devices + groups - 2)
     start_all(send.at[0], recv.at[0], 0)
+    inputs[2].wait()
+    inputs[3].wait()
     for j in range(blocks):
         at = columns_of(j)
         g_buf[j] = q_ref[:, at].astype(jnp.float32) * c_ref[:, at].astype(jnp.float32)
     pack(g_buf, 1)
     start_all(send.at[1], recv.at[1], 1)
-    for j in range(blocks):
-        wide[j] = h_ref[:, columns_of(j)]
+    for load in inputs[4:]:
+        load.wait()
     pack(wide, 2)
     start_all(send.at[2], recv.at[2], 2)
     for load in loads:
@@ -396,9 +410,16 @@
 
     wait_arrivals(back.at[0], home.at[0], 3)
     unpack(0)
+    for j in range(blocks):
+        dh_ref[:, columns_of(j)] = flat[0, j]
 
     wait_arrivals(back.at[1], home.at[1], 4)
     unpack(1)
+    for j in range(blocks):
+        at = columns_of(j)
+        inner = flat[1, j] + skip_ref[:, at] * x_buf[j]
+        out_ref[:, at] = (q_ref[:, at].astype(jnp.float32) * inner).astype(jnp.bfloat16)
+        dq_ref[:, at] = (c_ref[:, at].astype(jnp.float32) * inner).astype(jnp.bfloat16)
 
     for k in range(1, devices):
         tail_copy(k).wait_recv()
@@ -407,7 +428,7 @@
     for k in range(1, devices):
         total = total + tail_home[k, 1]
     total = jnp.sum(jnp.sum(total, axis=0, keepdims=True), axis=1, keepdims=True)
-    rms_ref[...] = total / count
+    rms_ref[...] = jnp.sqrt(total / count)
     for j in range(blocks):
         left = lax.broadcasted_iota(jnp.int32, (8, LANES), 1) < low
         both = jnp.where(left, tail_home[2 * j, 0], tail_home[2 * j + 1, 0])
@@ -415,6 +436,11 @@
 
     wait_arrivals(back.at[2], home.at[2], 5)
     unpack(2)
+    for j in range(blocks):
+        at = columns_of(j)
+        grad = flat[2, j] + skip_ref[:, at] * g_buf[j]
+        dk_ref[:, at] = (grad * v_ref[:, at].astype(jnp.float32)).astype(jnp.bfloat16)
+        dv_ref[:, at] = (grad * k_ref[:, at].astype(jnp.float32)).astype(jnp.bfloat16)
 
     for k in range(1, devices):
         for slot in range(3):
@@ -425,24 +451,16 @@
         square_copy(k).wait_send()
 
 
-def gate(
-    q_ref, k_ref, v_ref, c_ref, skip_ref, flat, direct_ref, mean_ref,
-    out_ref, dq_ref, dk_ref, dv_ref, dh_ref, dskip_ref, rms_ref,
-):
-    query_val = q_ref[...].astype(jnp.float32)
-    key_val = k_ref[...].astype(jnp.float32)
-    value_val = v_ref[...].astype(jnp.float32)
-    cot_val = c_ref[...].astype(jnp.float32)
-    skip = skip_ref[...]
-    inner = flat[1, 0] + skip * (key_val * value_val)
-    grad = flat[2, 0] + skip * (query_val * cot_val)
-    out_ref[...] = (query_val * inner).astype(jnp.bfloat16)
-    dq_ref[...] = (cot_val * inner).astype(jnp.bfloat16)
-    dk_ref[...] = (grad * value_val).astype(jnp.bfloat16)
-    dv_ref[...] = (grad * key_val).astype(jnp.bfloat16)
-    dh_ref[...] = flat[0, 0]
-    dskip_ref[...] = direct_ref[...]
-    rms_ref[...] = jnp.sqrt(mean_ref[...])
+def emit(*refs):
+    sources, targets, sem = refs[:7], refs[7:14], refs[14]
+    copies = [
+        pltpu.make_async_copy(source, target, sem.at[index])
+        for index, (source, target) in enumerate(zip(sources, targets))
+    ]
+    for copy in copies:
+        copy.start()
+    for copy in copies:
+        copy.wait()
 
 
 def fused_body(query_input, key_input, value_input, cotangent, filter_taps, skip_gain):
@@ -454,23 +472,29 @@
     tables, twists = half_tables(points)
     count = float(channels * groups * (rows * devices + 1))
     vmem = pl.BlockSpec(memory_space=pltpu.VMEM)
-    hbm = pl.BlockSpec(memory_space=pl.ANY)
-    narrow = jax.ShapeDtypeStruct((rows, channels), jnp.bfloat16)
+    hbm = pl.BlockSpec(memory_space=pltpu.HBM)
     moved = (3, devices, half, LANES)
     blocks = channels // LANES
-    flat, direct, rms = pl.pallas_call(
+    shapes = [((rows, channels), jnp.bfloat16)] * 4 + [
+        ((rows, channels), jnp.float32),
+        ((1, channels), jnp.float32),
+        ((1, 1), jnp.float32),
+    ]
+    held = pl.pallas_call(
         functools.partial(kernel, devices, groups, count),
-        out_shape=(
-            jax.ShapeDtypeStruct((3, blocks, rows, LANES), jnp.float32),
-            jax.ShapeDtypeStruct((1, channels), jnp.float32),
-            jax.ShapeDtypeStruct((1, 1), jnp.float32),
-        ),
-        in_specs=[vmem] * 5 + [hbm] * 2,
-        out_specs=(vmem,) * 3,
+        out_shape=tuple(pltpu.VMEM(*shape) for shape in shapes),
+        in_specs=[hbm] * 8,
+        out_specs=(vmem,) * 7,
         scratch_shapes=[
-            pltpu.VMEM((channels // LANES, rows, LANES), jnp.float32),
-            pltpu.VMEM((channels // LANES, rows, LANES), jnp.float32),
-            pltpu.VMEM((channels // LANES, rows, LANES), jnp.float32),
+            pltpu.VMEM((rows, channels), jnp.bfloat16),
+            pltpu.VMEM((rows, channels), jnp.bfloat16),
+            pltpu.VMEM((rows, channels), jnp.bfloat16),
+            pltpu.VMEM((rows, channels), jnp.bfloat16),
+            pltpu.VMEM((1, channels), jnp.float32),
+            pltpu.VMEM((blocks, rows, LANES), jnp.float32),
+            pltpu.VMEM((blocks, rows, LANES), jnp.float32),
+            pltpu.VMEM((blocks, rows, LANES), jnp.float32),
+            pltpu.VMEM((3, blocks, rows, LANES), jnp.float32),
             pltpu.VMEM(moved, jnp.float32),
             pltpu.VMEM(moved, jnp.float32),
             pltpu.VMEM((3, 2, points, LANES), jnp.float32),
@@ -491,33 +515,23 @@
             pltpu.SemaphoreType.DMA((groups,)),
             pltpu.SemaphoreType.DMA((groups,)),
             pltpu.SemaphoreType.DMA((4,)),
+            pltpu.SemaphoreType.DMA((5 + blocks,)),
         ],
-        compiler_params=pltpu.CompilerParams(collective_id=0, has_side_effects=True),
+        compiler_params=pltpu.CompilerParams(
+            collective_id=0, has_side_effects=True, vmem_limit_bytes=(64 << 20) - (960 << 10)
+        ),
     )(
-        query_input, key_input, value_input, cotangent, filter_taps, jnp.asarray(tables), jnp.asarray(twists),
-    )
-    column = pl.BlockSpec((rows, LANES), lambda j: (0, j))
-    line = pl.BlockSpec((1, LANES), lambda j: (0, j))
-    single = pl.BlockSpec((1, 1), lambda j: (0, 0))
+        query_input, key_input, value_input, cotangent, filter_taps,
+        skip_gain.reshape(1, channels), jnp.asarray(tables), jnp.asarray(twists),
+    )
     results = pl.pallas_call(
-        gate,
-        grid=(blocks,),
-        out_shape=(
-            narrow,
-            narrow,
-            narrow,
-            narrow,
-            jax.ShapeDtypeStruct((rows, channels), jnp.float32),
-            jax.ShapeDtypeStruct((1, channels), jnp.float32),
-            jax.ShapeDtypeStruct((1, 1), jnp.float32),
-        ),
-        in_specs=[column] * 4
-        + [line, pl.BlockSpec((3, 1, rows, LANES), lambda j: (0, j, 0, 0)), line, single],
-        out_specs=[column] * 5 + [line, single],
-    )(
-        query_input, key_input, value_input, cotangent,
-        skip_gain.reshape(1, channels), flat, direct, rms,
-    )
+        emit,
+        out_shape=tuple(jax.ShapeDtypeStruct(*shape) for shape in shapes),
+        in_specs=[vmem] * 7,
+        out_specs=(hbm,) * 7,
+        scratch_shapes=[pltpu.SemaphoreType.DMA((7,))],
+        compiler_params=pltpu.CompilerParams(vmem_limit_bytes=4 << 20),
+    )(*held)
     return (*results[:5], results[5].reshape(channels), results[6].reshape(()))
 
 

time: 50.6 us -> 46.7 us (0.923)
  Pallas kernels: 49.8 us -> 45.9 us
    pallas_call x1, Pallas kernels: 4.13 us -> 1.57 us  [fused_body(): pl.pallas_call(emit, out_shape=tuple((jax.ShapeDtypeStruct(*shape) for sh...]
    pallas_call x1, Pallas kernels: 45.7 us -> 44.3 us  [fused_body(): pl.pallas_call(functools.partial(kernel, devices, groups, count), out_sha...]
where the time goes in v1:
time: 46.7 us; the launch traced here: 46.5 us
  Pallas kernels  45.9 us (98%)
  between operations  0.64 us (1%)
    pallas_call x1, Pallas kernels, fused_body(): pl.pallas_call(functools.partial(kernel, devices, groups, count), out_sha...  44.3 us
    pallas_call x1, Pallas kernels, fused_body(): pl.pallas_call(emit, out_shape=tuple((jax.ShapeDtypeStruct(*shape) for sh...  1.57 us

profile of v1, /device:TPU:0, one launch (start us, length us, event | category | flops | bytes accessed | tf_op | source)
XLA Modules:
  0.0 46.5 jit_solution(17556127591527637246)
XLA Ops:
  0.6 44.3 %shard_map.135 = (bf16[128,512]{1,0:T(8,128)(2,1)S(1)}, bf16[128,512]{1,0:T(8,128)(2,1)S(1)}, bf16[128,512]{1,0:T(8,128)(2,1)S(1)}, bf16[128,512]{1,0:T(8,128)(2...) custom-call(bf16[128,512]{1,0:T(8,128)(2,1)} %q_hbm.1, bf16[128,512]{1,0:T(8,128)(2,1)} %k_hbm.1, ...), custom_call_target="tpu_custom_call" | custom-call | tf_op jit(solution)/shard_map/pallas_call | solution.py:483
  44.9 1.6 %shard_map.136 = (bf16[128,512]{1,0:T(8,128)(2,1)}, bf16[128,512]{1,0:T(8,128)(2,1)}, bf16[128,512]{1,0:T(8,128)(2,1)}, bf16[128,512]{1,0:T(8,128)(2,1)}, f32[12...) custom-call(bf16[128,512]{1,0:T(8,128)(2,1)S(1)} %get-tuple-element.21.refs_0_, ...), custom_call_target="tpu_custom_call" | custom-call | tf_op jit(solution)/shard_map/pallas_call | solution.py:527

commit v2 on v1

--- a/solution.py
+++ b/solution.py
@@ -184,8 +184,10 @@
     devices, groups, count,
     q_hbm, k_hbm, v_hbm, c_hbm, h_hbm, skip_hbm, table_hbm, twist_hbm,
     out_ref, dq_ref, dk_ref, dv_ref, dh_ref, dskip_ref, rms_ref,
-    q_ref, k_ref, v_ref, c_ref, skip_ref, x_buf, g_buf, wide, flat, send, recv, spec, prod, back, home, tail, tail_home, sq_send, sq_recv,
-    table, twist, send_sem, recv_sem, own_sem, tail_send, tail_recv, sq_ssem, sq_rsem, load_sem, in_sem,
+    q_ref, k_ref, v_ref, c_ref, skip_ref, x_buf, g_buf, wide, flat,
+    send, recv, spec, prod, back, home, extra, part_send, part_home, sq_send, sq_recv, sq_home,
+    table, twist, in_send, in_recv, out_send, home_recv, extra_recv,
+    part_ssem, part_rsem, sq_ssem, sq_rsem, tot_ssem, tot_rsem, load_sem, in_sem,
 ):
     me = lax.axis_index("seq")
     mine = lax.axis_index("ch")
@@ -194,6 +196,17 @@
     points = half * devices
     low = LANES // 2
     time_scale = 1.0 / math.sqrt(2 * points)
+    blocks = channels // LANES
+    side = devices // 2
+    pair = devices // 4
+    split = 3 * pair
+    base = me // side * side
+    other = side - base
+    early = me < side
+    late = me >= side
+    whole_here = (me >= pair) & (me < side)
+    far_second = (me >= side) & (me < split)
+    has_second = me < split
 
     barrier = pltpu.get_barrier_semaphore()
     for k in range(1, devices):
@@ -204,7 +217,6 @@
         pl.semaphore_signal(
             barrier, inc=1, device_id={"ch": lax.rem(mine + k, groups)}, device_id_type=MESH
         )
-    blocks = channels // LANES
 
     def columns_of(j):
         return pl.ds(j * LANES, LANES)
@@ -225,27 +237,145 @@
     for load in loads:
         load.start()
 
-    def remote(source, target, slot, k):
+    def near_owner(c):
+        return (c, 0) if c < pair else (c, 1) if c < side else (c - side, 1)
+
+    def far_owner(c):
+        return (side + c, 0) if c < side else (c, 1)
+
+    def whole_owner(c):
+        return (c - side, 0)
+
+    beyond = (me // pair + 3) // 4
+    my_chunk = (lax.rem(me + side * beyond, devices), me + side * (1 - beyond))
+
+    def to_owner(signal, c, owner, lane):
+        device, slot = owner
+        return pltpu.make_async_remote_copy(
+            src_ref=send.at[signal, c],
+            dst_ref=recv.at[slot, signal, me],
+            send_sem=in_send.at[signal, c, lane],
+            recv_sem=in_recv.at[slot, signal, me],
+            device_id={"seq": jnp.int32(device)},
+            device_id_type=MESH,
+        )
+
+    def give(signal, c, owner, lane, can_be_me):
+        device, slot = owner
+        if not can_be_me:
+            to_owner(signal, c, owner, lane).start()
+            return
+
+        @pl.when(me != device)
+        def _():
+            to_owner(signal, c, owner, lane).start()
+
+        @pl.when(me == device)
+        def _():
+            pltpu.make_async_copy(
+                send.at[signal, c], recv.at[slot, signal, me], in_recv.at[slot, signal, me]
+            ).start()
+
+    def given(signal, c, owner, lane, can_be_me):
+        if not can_be_me:
+            to_owner(signal, c, owner, lane).wait_send()
+            return
+
+        @pl.when(me != owner[0])
+        def _():
+            to_owner(signal, c, owner, lane).wait_send()
+
+    def early_far(signal, act):
+        for c in range(split):
+            act(signal, c, far_owner(c), 0, False)
+
+    def early_whole(signal, act):
+        for c in range(split, devices):
+            act(signal, c, whole_owner(c), 0, True)
+
+    def early_near(signal, act):
+        for c in range(split):
+            act(signal, c, near_owner(c), 1, True)
+
+    def late_all(signal, act):
+        for c in range(split, devices):
+            act(signal, c, whole_owner(c), 0, False)
+        for c in range(split):
+            act(signal, c, far_owner(c), 0, True)
+
+    def await_input(slot, signal):
+        def wait_from(start):
+            for k in range(side):
+                there = start + k
+                pltpu.make_async_copy(
+                    send.at[signal, 0], recv.at[slot, signal, there], in_recv.at[slot, signal, there]
+                ).wait()
+
+        wait_from(base)
+        if slot == 0:
+            crosses = whole_here if signal == 1 else me >= pair
+        elif signal == 1:
+            return
+        else:
+            crosses = far_second
+
+        @pl.when(crosses)
+        def _():
+            wait_from(other)
+
+    def to_home(slot, kind, dest):
+        c = my_chunk[slot]
+        return pltpu.make_async_remote_copy(
+            src_ref=back.at[slot, kind, dest],
+            dst_ref=home.at[kind, c],
+            send_sem=out_send.at[slot, kind, dest],
+            recv_sem=home_recv.at[kind, c],
+            device_id={"seq": dest},
+            device_id_type=MESH,
+        )
+
+    def to_extra(slot, kind, dest):
+        c = my_chunk[slot]
+        return pltpu.make_async_remote_copy(
+            src_ref=back.at[slot, kind, dest],
+            dst_ref=extra.at[kind, c],
+            send_sem=out_send.at[slot, kind, dest],
+            recv_sem=extra_recv.at[kind, c],
+            device_id={"seq": dest},
+            device_id_type=MESH,
+        )
+
+    def outward(slot, kind, act):
+        if slot == 0:
+            @pl.when(whole_here)
+            def _():
+                for k in range(side):
+                    act(to_home(slot, kind, other + k))
+
+        if kind < 2:
+            @pl.when(late if slot == 0 else far_second)
+            def _():
+                for k in range(side):
+                    act(to_extra(slot, kind, other + k))
+
+        for k in range(1, side):
+            act(to_home(slot, kind, base + lax.rem(me - base + k, side)))
+
+    def give_back(slot, kind):
+        outward(slot, kind, lambda copy: copy.start())
+        c = my_chunk[slot]
+        pltpu.make_async_copy(back.at[slot, kind, me], home.at[kind, c], home_recv.at[kind, c]).start()
+
+    def given_back(slot, kind):
+        outward(slot, kind, lambda copy: copy.wait_send())
+
+    def part_copy(k):
         peer = lax.rem(me + k, devices)
         return pltpu.make_async_remote_copy(
-            src_ref=source.at[peer],
-            dst_ref=target.at[me],
-            send_sem=send_sem.at[slot, k],
-            recv_sem=recv_sem.at[slot, k],
-            device_id={"seq": peer},
-            device_id_type=MESH,
-        )
-
-    def own(source, target, slot):
-        return pltpu.make_async_copy(source.at[me], target.at[me], own_sem.at[slot])
-
-    def tail_copy(k):
-        peer = lax.rem(me + k, devices)
-        return pltpu.make_async_remote_copy(
-            src_ref=tail,
-            dst_ref=tail_home.at[me],
-            send_sem=tail_send.at[k],
-            recv_sem=tail_recv.at[k],
+            src_ref=part_send,
+            dst_ref=part_home.at[me],
+            send_sem=part_ssem.at[k],
+            recv_sem=part_rsem.at[k],
             device_id={"seq": peer},
             device_id_type=MESH,
         )
@@ -253,7 +383,7 @@
     def square_copy(k):
         peer = lax.rem(mine + k, groups)
         return pltpu.make_async_remote_copy(
-            src_ref=sq_send,
+            src_ref=sq_send.at[0],
             dst_ref=sq_recv.at[mine],
             send_sem=sq_ssem.at[k],
             recv_sem=sq_rsem.at[k],
@@ -261,35 +391,25 @@
             device_id_type=MESH,
         )
 
-    def start_all(source, target, slot):
-        for k in range(1, devices):
-            remote(source, target, slot, k).start()
-        own(source, target, slot).start()
-
-    def wait_arrivals(source, target, slot):
-        for k in range(1, devices):
-            remote(source, target, slot, k).wait_recv()
-        own(source, target, slot).wait()
+    def total_copy(k):
+        peer = lax.rem(me + k, devices)
+        return pltpu.make_async_remote_copy(
+            src_ref=sq_send.at[1],
+            dst_ref=sq_home.at[me],
+            send_sem=tot_ssem.at[k],
+            recv_sem=tot_rsem.at[k],
+            device_id={"seq": peer},
+            device_id_type=MESH,
+        )
 
     first = lax.broadcasted_iota(jnp.int32, (half, LANES), 1) < low
 
     def pack(source, signal):
-        for j in range(channels // LANES):
+        for j in range(blocks):
             even = source[j, pl.ds(0, half, stride=2), :]
             odd = source[j, pl.ds(1, half, stride=2), :]
             send[signal, 2 * j] = jnp.where(first, even, pltpu.roll(odd, low, 1))
             send[signal, 2 * j + 1] = jnp.where(first, pltpu.roll(even, low, 1), odd)
-
-    def unpack(signal):
-        for j in range(channels // LANES):
-            left = home[signal, 2 * j]
-            right = home[signal, 2 * j + 1]
-            flat[signal, j, pl.ds(0, half, stride=2), :] = jnp.where(
-                first, left, pltpu.roll(right, low, 1)
-            )
-            flat[signal, j, pl.ds(1, half, stride=2), :] = jnp.where(
-                first, pltpu.roll(left, low, 1), right
-            )
 
     inputs[0].wait()
     inputs[1].wait()
@@ -298,18 +418,71 @@
         x_buf[j] = k_ref[:, at].astype(jnp.float32) * v_ref[:, at].astype(jnp.float32)
     pack(x_buf, 0)
     pl.semaphore_wait(barrier, devices + groups - 2)
-    start_all(send.at[0], recv.at[0], 0)
+
+    @pl.when(early)
+    def _():
+        early_far(0, give)
+        early_whole(0, give)
+
+    @pl.when(late)
+    def _():
+        late_all(0, give)
+
     inputs[2].wait()
     inputs[3].wait()
     for j in range(blocks):
         at = columns_of(j)
         g_buf[j] = q_ref[:, at].astype(jnp.float32) * c_ref[:, at].astype(jnp.float32)
     pack(g_buf, 1)
-    start_all(send.at[1], recv.at[1], 1)
+
+    @pl.when(early)
+    def _():
+        early_whole(1, give)
+
+    @pl.when(late)
+    def _():
+        late_all(1, give)
+
     for load in inputs[4:]:
         load.wait()
     pack(wide, 2)
-    start_all(send.at[2], recv.at[2], 2)
+
+    @pl.when(early)
+    def _():
+        early_far(2, give)
+        early_whole(2, give)
+        for signal in range(3):
+            early_near(signal, give)
+
+    @pl.when(late)
+    def _():
+        late_all(2, give)
+
+    part_send[...] = jnp.zeros((8, LANES), jnp.float32)
+    for j in range(blocks):
+        part_send[pl.ds(j, 1), :] = jnp.sum(x_buf[j] * g_buf[j], axis=0, keepdims=True) * time_scale
+    part_home[me] = part_send[...]
+    for k in range(1, devices):
+        part_copy(k).start()
+
+    nothing = jnp.zeros((side, half, LANES), jnp.float32)
+
+    @pl.when(me < pair)
+    def _():
+        for signal in range(3):
+            recv[0, signal, pl.ds(side, side)] = nothing
+
+    @pl.when(early)
+    def _():
+        for signal in range(3):
+            recv[1, signal, pl.ds(side, side)] = nothing
+
+    @pl.when(late)
+    def _():
+        recv[0, 1, pl.ds(0, side)] = nothing
+        recv[1, 1, pl.ds(0, side)] = nothing
+        extra[...] = jnp.zeros(extra.shape, jnp.float32)
+
     for load in loads:
         load.wait()
 
@@ -319,28 +492,26 @@
         small = jnp.dot(table[2 * which + 1], high, preferred_element_type=jnp.float32)
         return main[:, :LANES] + (main[:, LANES:] + small)
 
-    def forward(signal):
-        high, rest = split_high_low(recv[signal].reshape(points, LANES))
-        spec[signal, 0] = times(0, high, rest)
-        spec[signal, 1] = -times(1, high, rest)
-
-    def inverse(slot, scale):
+    def forward(slot, signal):
+        high, rest = split_high_low(recv[slot, signal].reshape(points, LANES))
+        spec[slot, signal, 0] = times(0, high, rest)
+        spec[slot, signal, 1] = -times(1, high, rest)
+
+    def inverse(slot, kind, scale):
         real_high, real_rest = split_high_low(prod[0])
         imag_high, imag_rest = split_high_low(prod[1])
         series = times(0, real_high, real_rest) - times(1, imag_high, imag_rest)
-        series = series * (scale / points)
-        back[slot] = series.reshape(devices, half, LANES)
-        return series
-
-    step = 32
-
-    def halves(ref_row, part, at):
-        value = spec[ref_row, part, at, :]
+        back[slot, kind] = (series * (scale / points)).reshape(devices, half, LANES)
+
+    step = 128
+
+    def halves(slot, ref_row, part, at):
+        value = spec[slot, ref_row, part, at, :]
         turned = pltpu.roll(value, low, 1)
         left = lax.broadcasted_iota(jnp.int32, (step, LANES), 1) < low
         return value, turned, jnp.where(left, value, turned), jnp.where(left, turned, value)
 
-    def products(signal, other, conjugate):
+    def products(slot, signal, other_signal, conjugate):
         sign = jnp.where(lax.broadcasted_iota(jnp.int32, (step, LANES), 1) < low, 1.0, -1.0)
 
         @pl.loop(0, points // step)
@@ -349,10 +520,10 @@
             cosine = twist[0, at, :]
             sine = twist[1, at, :]
             signed = sine * sign
-            _, _, even_re, odd_re = halves(other, 0, at)
-            _, _, even_im, odd_im = halves(other, 1, at)
-            a_re, as_re, _, _ = halves(signal, 0, at)
-            a_im, as_im, _, _ = halves(signal, 1, at)
+            _, _, even_re, odd_re = halves(slot, other_signal, 0, at)
+            _, _, even_im, odd_im = halves(slot, other_signal, 1, at)
+            a_re, as_re, _, _ = halves(slot, signal, 0, at)
+            a_im, as_im, _, _ = halves(slot, signal, 1, at)
             p_re = even_re * cosine - even_im * sine
             p_im = even_im * cosine + even_re * sine
             if conjugate:
@@ -366,89 +537,142 @@
                 prod[0, at, :] = a_re * p_re - a_im * p_im + (as_re * r_re - as_im * r_im)
                 prod[1, at, :] = a_im * p_re + a_re * p_im + (as_im * r_re + as_re * r_im)
 
-    wait_arrivals(send.at[0], recv.at[0], 0)
-    forward(0)
-    wait_arrivals(send.at[1], recv.at[1], 1)
-    forward(1)
-    products(1, 0, True)
-    series = inverse(0, time_scale)
-    start_all(back.at[0], home.at[0], 3)
-    direct = jnp.sum(
-        (recv[0] * recv[1]).reshape(points // 8, 8, LANES), axis=0
-    )
-    direct = jnp.sum(direct, axis=0, keepdims=True)
-    direct = jnp.broadcast_to(direct, (8, LANES)) * time_scale
-    direct = direct + pltpu.roll(direct, low, 1)
-    squares = jnp.sum((series * series).reshape(points // 8, 8, LANES), axis=0)
-    squares = squares + direct * direct * (1.0 / 16.0)
-    sq_send[...] = squares
+    def begin(slot):
+        await_input(slot, 0)
+        forward(slot, 0)
+        await_input(slot, 1)
+        forward(slot, 1)
+        products(slot, 1, 0, True)
+        inverse(slot, 0, time_scale)
+        give_back(slot, 0)
+
+    def finish(slot):
+        await_input(slot, 2)
+        forward(slot, 2)
+        products(slot, 1, 2, True)
+        inverse(slot, 1, 1.0)
+        give_back(slot, 1)
+        products(slot, 0, 2, False)
+        inverse(slot, 2, 1.0)
+        give_back(slot, 2)
+
+    begin(0)
+
+    @pl.when(has_second)
+    def _():
+        begin(1)
+
+    finish(0)
+
+    @pl.when(has_second)
+    def _():
+        finish(1)
+
+    def await_home(kind, c):
+        pltpu.make_async_copy(back.at[0, 0, 0], home.at[kind, c], home_recv.at[kind, c]).wait()
+
+    def await_extra(kind, c):
+        pltpu.make_async_copy(back.at[0, 0, 0], extra.at[kind, c], extra_recv.at[kind, c]).wait()
+
+    def unpack(kind, j):
+        pieces = []
+        for c in (2 * j, 2 * j + 1):
+            await_home(kind, c)
+        if kind < 2 and 2 * j < split:
+            @pl.when(early)
+            def _():
+                for c in (2 * j, 2 * j + 1):
+                    await_extra(kind, c)
+
+            pieces = [home[kind, c] + extra[kind, c] for c in (2 * j, 2 * j + 1)]
+        else:
+            pieces = [home[kind, c] for c in (2 * j, 2 * j + 1)]
+        left, right = pieces
+        flat[j, pl.ds(0, half, stride=2), :] = jnp.where(first, left, pltpu.roll(right, low, 1))
+        flat[j, pl.ds(1, half, stride=2), :] = jnp.where(first, pltpu.roll(left, low, 1), right)
+        return flat[j]
+
+    for k in range(1, devices):
+        part_copy(k).wait_recv()
+    direct = part_home[0]
+    for k in range(1, devices):
+        direct = direct + part_home[k]
+    for j in range(blocks):
+        dskip_ref[:, columns_of(j)] = direct[j : j + 1]
+
+    squares = direct * direct * (1.0 / devices)
+    for j in reversed(range(blocks)):
+        value = unpack(0, j)
+        dh_ref[:, columns_of(j)] = value
+        squares = squares + jnp.sum((value * value).reshape(rows // 8, 8, LANES), axis=0)
+    sq_send[0] = squares
+    sq_recv[mine] = squares
     for k in range(1, groups):
         square_copy(k).start()
-    sq_own = pltpu.make_async_copy(sq_send, sq_recv.at[mine], load_sem.at[2])
-    sq_own.start()
-
-    wait_arrivals(send.at[2], recv.at[2], 2)
-    forward(2)
-    products(0, 2, False)
-    inverse(1, 1.0)
-    start_all(back.at[1], home.at[1], 4)
+
+    @pl.when(early)
+    def _():
+        early_far(0, given)
+        early_far(2, given)
+        for signal in range(3):
+            early_whole(signal, given)
+            early_near(signal, given)
+
+    @pl.when(late)
+    def _():
+        for signal in range(3):
+            late_all(signal, given)
+
+    for k in range(1, devices):
+        part_copy(k).wait_send()
+
+    given_back(0, 0)
+
+    @pl.when(has_second)
+    def _():
+        given_back(1, 0)
+
     for k in range(1, groups):
         square_copy(k).wait_recv()
-    sq_own.wait()
     total = sq_recv[0]
     for k in range(1, groups):
         total = total + sq_recv[k]
-    tail[0] = direct
-    tail[1] = total
-    for k in range(1, devices):
-        tail_copy(k).start()
-    tail_own = pltpu.make_async_copy(tail, tail_home.at[me], load_sem.at[3])
-    tail_own.start()
-    products(1, 2, True)
-    inverse(2, 1.0)
-    start_all(back.at[2], home.at[2], 5)
-
-    wait_arrivals(back.at[0], home.at[0], 3)
-    unpack(0)
-    for j in range(blocks):
-        dh_ref[:, columns_of(j)] = flat[0, j]
-
-    wait_arrivals(back.at[1], home.at[1], 4)
-    unpack(1)
-    for j in range(blocks):
+    sq_send[1] = total
+    sq_home[me] = total
+    for k in range(1, devices):
+        total_copy(k).start()
+
+    for j in reversed(range(blocks)):
         at = columns_of(j)
-        inner = flat[1, j] + skip_ref[:, at] * x_buf[j]
+        inner = unpack(2, j) + skip_ref[:, at] * x_buf[j]
         out_ref[:, at] = (q_ref[:, at].astype(jnp.float32) * inner).astype(jnp.bfloat16)
         dq_ref[:, at] = (c_ref[:, at].astype(jnp.float32) * inner).astype(jnp.bfloat16)
 
     for k in range(1, devices):
-        tail_copy(k).wait_recv()
-    tail_own.wait()
-    total = tail_home[0, 1]
-    for k in range(1, devices):
-        total = total + tail_home[k, 1]
+        total_copy(k).wait_recv()
+    total = sq_home[0]
+    for k in range(1, devices):
+        total = total + sq_home[k]
     total = jnp.sum(jnp.sum(total, axis=0, keepdims=True), axis=1, keepdims=True)
     rms_ref[...] = jnp.sqrt(total / count)
-    for j in range(blocks):
-        left = lax.broadcasted_iota(jnp.int32, (8, LANES), 1) < low
-        both = jnp.where(left, tail_home[2 * j, 0], tail_home[2 * j + 1, 0])
-        dskip_ref[:, columns_of(j)] = both[0:1]
-
-    wait_arrivals(back.at[2], home.at[2], 5)
-    unpack(2)
-    for j in range(blocks):
+    for k in range(1, groups):
+        square_copy(k).wait_send()
+    for k in range(1, devices):
+        total_copy(k).wait_send()
+
+    for j in reversed(range(blocks)):
         at = columns_of(j)
-        grad = flat[2, j] + skip_ref[:, at] * g_buf[j]
+        grad = unpack(1, j) + skip_ref[:, at] * g_buf[j]
         dk_ref[:, at] = (grad * v_ref[:, at].astype(jnp.float32)).astype(jnp.bfloat16)
         dv_ref[:, at] = (grad * k_ref[:, at].astype(jnp.float32)).astype(jnp.bfloat16)
 
-    for k in range(1, devices):
-        for slot in range(3):
-            remote(send.at[slot], recv.at[slot], slot, k).wait_send()
-            remote(back.at[slot], home.at[slot], slot + 3, k).wait_send()
-        tail_copy(k).wait_send()
-    for k in range(1, groups):
-        square_copy(k).wait_send()
+    for kind in (1, 2):
+        given_back(0, kind)
+
+    @pl.when(has_second)
+    def _():
+        for kind in (1, 2):
+            given_back(1, kind)
 
 
 def emit(*refs):
@@ -473,7 +697,7 @@
     count = float(channels * groups * (rows * devices + 1))
     vmem = pl.BlockSpec(memory_space=pltpu.VMEM)
     hbm = pl.BlockSpec(memory_space=pltpu.HBM)
-    moved = (3, devices, half, LANES)
+    chunks = 2 * channels // LANES
     blocks = channels // LANES
     shapes = [((rows, channels), jnp.bfloat16)] * 4 + [
         ((rows, channels), jnp.float32),
@@ -494,27 +718,33 @@
             pltpu.VMEM((blocks, rows, LANES), jnp.float32),
             pltpu.VMEM((blocks, rows, LANES), jnp.float32),
             pltpu.VMEM((blocks, rows, LANES), jnp.float32),
-            pltpu.VMEM((3, blocks, rows, LANES), jnp.float32),
-            pltpu.VMEM(moved, jnp.float32),
-            pltpu.VMEM(moved, jnp.float32),
-            pltpu.VMEM((3, 2, points, LANES), jnp.float32),
+            pltpu.VMEM((blocks, rows, LANES), jnp.float32),
+            pltpu.VMEM((3, chunks, half, LANES), jnp.float32),
+            pltpu.VMEM((2, 3, devices, half, LANES), jnp.float32),
+            pltpu.VMEM((2, 3, 2, points, LANES), jnp.float32),
             pltpu.VMEM((2, points, LANES), jnp.float32),
-            pltpu.VMEM(moved, jnp.float32),
-            pltpu.VMEM(moved, jnp.float32),
+            pltpu.VMEM((2, 3, devices, half, LANES), jnp.float32),
+            pltpu.VMEM((3, chunks, half, LANES), jnp.float32),
+            pltpu.VMEM((2, 3 * (devices // 4), half, LANES), jnp.float32),
+            pltpu.VMEM((8, LANES), jnp.float32),
+            pltpu.VMEM((devices, 8, LANES), jnp.float32),
             pltpu.VMEM((2, 8, LANES), jnp.float32),
-            pltpu.VMEM((devices, 2, 8, LANES), jnp.float32),
-            pltpu.VMEM((8, LANES), jnp.float32),
             pltpu.VMEM((groups, 8, LANES), jnp.float32),
+            pltpu.VMEM((devices, 8, LANES), jnp.float32),
             pltpu.VMEM(tables.shape, jnp.bfloat16),
             pltpu.VMEM(twists.shape, jnp.float32),
-            pltpu.SemaphoreType.DMA((6, devices)),
-            pltpu.SemaphoreType.DMA((6, devices)),
-            pltpu.SemaphoreType.DMA((6,)),
+            pltpu.SemaphoreType.DMA((3, chunks, 2)),
+            pltpu.SemaphoreType.DMA((2, 3, devices)),
+            pltpu.SemaphoreType.DMA((2, 3, devices)),
+            pltpu.SemaphoreType.DMA((3, chunks)),
+            pltpu.SemaphoreType.DMA((2, 3 * (devices // 4))),
             pltpu.SemaphoreType.DMA((devices,)),
             pltpu.SemaphoreType.DMA((devices,)),
             pltpu.SemaphoreType.DMA((groups,)),
             pltpu.SemaphoreType.DMA((groups,)),
-            pltpu.SemaphoreType.DMA((4,)),
+            pltpu.SemaphoreType.DMA((devices,)),
+            pltpu.SemaphoreType.DMA((devices,)),
+            pltpu.SemaphoreType.DMA((2,)),
             pltpu.SemaphoreType.DMA((5 + blocks,)),
         ],
         compiler_params=pltpu.CompilerParams(
@@ -538,7 +768,7 @@
 def pick_body(query_input, *others):
     devices = lax.axis_size("seq")
     rows, channels = query_input.shape
-    fits = 2 * channels == LANES * devices and channels % LANES == 0 and rows % 16 == 0
+    fits = devices == 8 and 2 * channels == LANES * devices and rows % 16 == 0
     chosen = fused_body if fits and rows * devices <= 2048 else body
     return chosen(query_input, *others)
 

time: 46.7 us -> 45.7 us (0.979)
  Pallas kernels: 45.9 us -> 44.9 us
    pallas_call x1, Pallas kernels: 44.3 us -> 43.3 us  [fused_body(): pl.pallas_call(functools.partial(kernel, devices, groups, count), out_sha...]
where the time goes in v2:
time: 45.7 us; the launch traced here: 45.5 us
  Pallas kernels  44.9 us (98%)
  between operations  0.64 us (1%)
    pallas_call x1, Pallas kernels, fused_body(): pl.pallas_call(functools.partial(kernel, devices, groups, count), out_sha...  43.3 us
    pallas_call x1, Pallas kernels, fused_body(): pl.pallas_call(emit, out_shape=tuple((jax.ShapeDtypeStruct(*shape) for sh...  1.57 us

profile of v2, /device:TPU:0, one launch (start us, length us, event | category | flops | bytes accessed | tf_op | source)
XLA Modules:
  0.0 45.5 jit_solution(2267902278261760279)
XLA Ops:
  0.6 43.3 %shard_map.135 = (bf16[128,512]{1,0:T(8,128)(2,1)S(1)}, bf16[128,512]{1,0:T(8,128)(2,1)S(1)}, bf16[128,512]{1,0:T(8,128)(2,1)S(1)}, bf16[128,512]{1,0:T(8,128)(2...) custom-call(bf16[128,512]{1,0:T(8,128)(2,1)} %q_hbm.1, bf16[128,512]{1,0:T(8,128)(2,1)} %k_hbm.1, ...), custom_call_target="tpu_custom_call" | custom-call | tf_op jit(solution)/shard_map/pallas_call | solution.py:707
  43.9 1.6 %shard_map.136 = (bf16[128,512]{1,0:T(8,128)(2,1)}, bf16[128,512]{1,0:T(8,128)(2,1)}, bf16[128,512]{1,0:T(8,128)(2,1)}, bf16[128,512]{1,0:T(8,128)(2,1)}, f32[12...) custom-call(bf16[128,512]{1,0:T(8,128)(2,1)S(1)} %get-tuple-element.21.refs_0_, ...), custom_call_target="tpu_custom_call" | custom-call | tf_op jit(solution)/shard_map/pallas_call | solution.py:757

commit v3 on v1

v3 whole, which is shorter than its diff:
```python
import functools
import math

import jax
import jax.numpy as jnp
import numpy as np
from jax import lax
from jax.experimental import pallas as pl
from jax.experimental.pallas import tpu as pltpu
from jax.sharding import PartitionSpec as P

LANES = 128
MESH = pl.DeviceIdType.MESH


def complex_mul(left_op, right_op):
    return jnp.stack(
        [
            left_op[0] * right_op[0] - left_op[1] * right_op[1],
            left_op[0] * right_op[1] + left_op[1] * right_op[0],
        ]
    )


def conj_of(stacked):
    return jnp.stack([stacked[0], -stacked[1]])


def dft_table(length, direction):
    counter = jnp.arange(length)
    angles = (
        2.0 * math.pi / length * (counter[:, None] * counter[None, :] % length).astype(jnp.float32)
    )
    return (jnp.cos(angles), direction * jnp.sin(angles))


def dft_along(stacked, length, direction, pattern):
    table_re, table_im = dft_table(length, direction)

    def contract(table, part_in):
        return jnp.einsum(pattern, table, part_in, precision=lax.Precision.HIGHEST)

    real_out = contract(table_re, stacked[0]) - contract(table_im, stacked[1])
    imag_out = contract(table_re, stacked[1]) + contract(table_im, stacked[0])
    return jnp.stack([real_out, imag_out])


def grid_twiddle(devices, block, direction):
    seq_length = devices * block
    counter = jnp.arange(devices)[:, None] * jnp.arange(block)[None, :] % seq_length
    angles = direction * 2.0 * math.pi / seq_length * counter.astype(jnp.float32)
    return jnp.stack([jnp.cos(angles), jnp.sin(angles)])[:, None, None]


def local_forward(stacked, devices, block):
    array_shape = stacked.shape
    stacked = stacked.reshape(array_shape[0], array_shape[1], array_shape[2], devices, block)
    stacked = dft_along(stacked, devices, -1.0, "kj,scjp->sckp")
    stacked = complex_mul(stacked, grid_twiddle(devices, block, -1.0))
    return dft_along(stacked, block, -1.0, "kp,scjp->scjk")


def local_inverse(stacked, devices, block):
    stacked = dft_along(stacked, block, 1.0, "kp,scjp->scjk")
    stacked = complex_mul(stacked, grid_twiddle(devices, block, 1.0))
    stacked = dft_along(stacked, devices, 1.0, "kj,scjp->sckp")
    array_shape = stacked.shape
    return stacked.reshape(array_shape[0], array_shape[1], array_shape[2], devices * block) / (
        devices * block
    )


def modulated(signals, cosine, sine_part):
    zero_part = jnp.zeros_like(signals)
    return jnp.stack(
        [
            jnp.concatenate([signals, signals * cosine]),
            jnp.concatenate([zero_part, -signals * sine_part]),
        ]
    )


def spectral_products(spectrum):
    mixed_spec = spectrum[:, 0::3]
    gated_spec = spectrum[:, 1::3]
    taps_spec = spectrum[:, 2::3]
    out_spec = complex_mul(mixed_spec, taps_spec)
    back_spec = complex_mul(gated_spec, conj_of(taps_spec))
    grad_spec = complex_mul(gated_spec, conj_of(mixed_spec))
    return jnp.stack(
        [
            out_spec[:, 0],
            back_spec[:, 0],
            grad_spec[:, 0],
            out_spec[:, 1],
            back_spec[:, 1],
            grad_spec[:, 1],
        ],
        axis=1,
    )


def unfold(series, cosine, sine_part):
    return tuple(
        (
            0.5
            * (
                series[0, signal_index]
                + cosine * series[0, signal_index + 3]
                - sine_part * series[1, signal_index + 3]
            )
            for signal_index in range(3)
        )
    )


def channel_local(mixed_in, gated_cot, filter_taps, devices):
    pieces = (
        lax.all_to_all(mixed_in, "seq", split_axis=1, concat_axis=0, tiled=True),
        lax.all_to_all(gated_cot, "seq", split_axis=1, concat_axis=0, tiled=True),
        lax.all_to_all(filter_taps, "seq", split_axis=1, concat_axis=0, tiled=True),
    )
    laid = jnp.transpose(jnp.stack(pieces), (0, 2, 1))
    seq_length = laid.shape[2]
    block = seq_length // devices
    angles = math.pi / seq_length * jnp.arange(seq_length).astype(jnp.float32)
    cosine = jnp.cos(angles)
    sine_row = jnp.sin(angles)
    spectrum = local_forward(modulated(laid, cosine, sine_row), devices, block)
    series = local_inverse(spectral_products(spectrum), devices, block)
    results = unfold(series, cosine, sine_row)
    return (
        lax.all_to_all(results[0].T, "seq", split_axis=0, concat_axis=1, tiled=True),
        lax.all_to_all(results[1].T, "seq", split_axis=0, concat_axis=1, tiled=True),
        lax.all_to_all(results[2].T, "seq", split_axis=0, concat_axis=1, tiled=True),
    )


def body(query_input, key_input, value_input, cotangent, filter_taps, skip_gain):
    devices = lax.axis_size("seq")
    row_count, channels = query_input.shape
    seq_length = row_count * devices
    query_val = query_input.astype(jnp.float32)
    key_val = key_input.astype(jnp.float32)
    value_val = value_input.astype(jnp.float32)
    cot_val = cotangent.astype(jnp.float32)
    mixed_in = key_val * value_val
    gated_cot = query_val * cot_val
    conv_out, back_conv, kernel_grad = channel_local(mixed_in, gated_cot, filter_taps, devices)
    inner_sum = conv_out + skip_gain[None, :] * mixed_in
    mixed_grad = back_conv + skip_gain[None, :] * gated_cot
    output = (query_val * inner_sum).astype(jnp.bfloat16)
    query_grad = (cot_val * inner_sum).astype(jnp.bfloat16)
    key_grad = (mixed_grad * value_val).astype(jnp.bfloat16)
    value_grad = (mixed_grad * key_val).astype(jnp.bfloat16)
    time_scale = 1.0 / math.sqrt(seq_length)
    filter_grad = kernel_grad * time_scale
    filter_sq = jnp.sum(filter_grad * filter_grad)
    skip_part = jnp.sum(gated_cot * mixed_in, axis=0) * time_scale
    skip_grad = lax.psum(skip_part, "seq")
    total_sq = lax.psum(filter_sq + jnp.sum(skip_grad * skip_grad) / devices, ("seq", "ch"))
    grad_rms = jnp.sqrt(total_sq / (channels * lax.axis_size("ch") * (seq_length + 1)))
    return (output, query_grad, key_grad, value_grad, filter_grad, skip_grad, grad_rms)


def split_high_low(array):
    high = array.astype(jnp.bfloat16)
    return high, (array - high.astype(jnp.float32)).astype(jnp.bfloat16)


def half_tables(points):
    odd = 2 * np.arange(points, dtype=np.int64) + 1
    angles = math.pi / (4 * points) * (odd[:, None] * odd[None, :] % (8 * points))
    parts = []
    for table in (np.cos(angles), np.sin(angles)):
        table = table.astype(np.float32)
        high = table.astype(jnp.bfloat16)
        parts += [high, (table - high.astype(np.float32)).astype(jnp.bfloat16)]
    shift = math.pi / (4 * points) * odd[:, None] * np.ones((1, LANES))
    return np.stack(parts), np.stack([np.cos(shift), np.sin(shift)]).astype(np.float32)


def kernel(
    devices, groups, count,
    k_hbm, v_hbm, q_hbm, c_hbm, h_hbm, skip_hbm, table_hbm, twist_hbm,
    out_ref, dq_ref, dk_ref, dv_ref, dh_ref, dskip_ref, rms_ref,
    gates, skip_ref, x_buf, g_buf, wide, flat,
    send, recv, spec, prod, back, home, extra,
    part_send, part_home, sq_acc, sq_send, sq_recv, sq_home, table, twist,
    load_sem, in_send, in_recv, out_send, home_recv, extra_recv, small_send, small_recv,
):
    me = lax.axis_index("seq")
    mine = lax.axis_index("ch")
    rows, channels = q_hbm.shape
    half = rows // 2
    points = half * devices
    low = LANES // 2
    time_scale = 1.0 / math.sqrt(2 * points)
    blocks = channels // LANES
    side = devices // 2
    pair = devices // 4
    split = 3 * pair
    base = me // side * side
    other = side - base
    early = me < side
    late = me >= side
    near_here = me < pair
    whole_here = (me >= pair) & (me < side)
    far_two = (me >= side) & (me < split)
    far_one = me >= split

    barrier = pltpu.get_barrier_semaphore()
    for k in range(1, devices):
        pl.semaphore_signal(
            barrier, inc=1, device_id={"seq": lax.rem(me + k, devices)}, device_id_type=MESH
        )
    for k in range(1, groups):
        pl.semaphore_signal(
            barrier, inc=1, device_id={"ch": lax.rem(mine + k, groups)}, device_id_type=MESH
        )

    def columns_of(j):
        return pl.ds(j * LANES, LANES)

    for index, source in enumerate((k_hbm, v_hbm, q_hbm, c_hbm)):
        pltpu.make_async_copy(source, gates.at[index], load_sem.at[index // 2]).start()
    for j in range(blocks):
        pltpu.make_async_copy(h_hbm.at[:, columns_of(j)], wide.at[j], load_sem.at[2]).start()
    loads = (
        pltpu.make_async_copy(skip_hbm, skip_ref, load_sem.at[3]),
        pltpu.make_async_copy(table_hbm, table, load_sem.at[4]),
        pltpu.make_async_copy(twist_hbm, twist, load_sem.at[5]),
    )
    for load in loads:
        load.start()

    def gate(index, j):
        return gates[index, :, columns_of(j)].astype(jnp.float32)

    def wait_bytes(ref, sem):
        pltpu.make_async_copy(ref, ref, sem).wait()

    def near_owner(c):
        return (c % pair, c // pair)

    def far_owner(c):
        return (side + c, 0) if c < side else (c, 1)

    def whole_owner(c):
        return (c - side, 0)

    def give(signal, c, owner, can_be_me):
        device, slot = owner
        target = recv.at[(slot * 3 + signal) * devices + me]
        sem = in_recv.at[slot * 3 + signal]

        def remote():
            pltpu.make_async_remote_copy(
                src_ref=send.at[signal, c],
                dst_ref=target,
                send_sem=in_send.at[0],
                recv_sem=sem,
                device_id={"seq": jnp.int32(device)},
                device_id_type=MESH,
            ).start()

        if not can_be_me:
            remote()
            return

        pl.when(me != device)(remote)

        @pl.when(me == device)
        def _():
            pltpu.make_async_copy(send.at[signal, c], target, sem).start()

    def give_far(signal, chunks, can_be_me=False):
        for c in chunks:
            give(signal, c, far_owner(c), can_be_me)

    def give_whole(signal, can_be_me=False):
        for c in range(split, devices):
            give(signal, c, whole_owner(c), can_be_me)

    def give_near(signal, slot, can_be_me=False):
        for c in range(slot * pair, (slot + 1) * pair):
            give(signal, c, near_owner(c), can_be_me)

    def await_input(slot, signal, start, sources):
        first_one = (slot * 3 + signal) * devices + start
        wait_bytes(recv.at[pl.ds(first_one, sources)], in_recv.at[slot * 3 + signal])

    def to_home(slot, kind, c, dest):
        pltpu.make_async_remote_copy(
            src_ref=back.at[slot, kind, dest],
            dst_ref=home.at[kind, c],
            send_sem=out_send.at[0],
            recv_sem=home_recv.at[kind],
            device_id={"seq": dest},
            device_id_type=MESH,
        ).start()

    def to_extra(slot, kind, c, dest):
        pltpu.make_async_remote_copy(
            src_ref=back.at[slot, kind, dest],
            dst_ref=extra.at[kind, c],
            send_sem=out_send.at[0],
            recv_sem=extra_recv.at[kind],
            device_id={"seq": dest},
            device_id_type=MESH,
        ).start()

    def inward(slot, kind, c):
        for k in range(1, side):
            to_home(slot, kind, c, base + lax.rem(me - base + k, side))
        pltpu.make_async_copy(back.at[slot, kind, me], home.at[kind, c], home_recv.at[kind]).start()

    def small_copy(source, target, index, device_id):
        return pltpu.make_async_remote_copy(
            src_ref=source,
            dst_ref=target,
            send_sem=small_send.at[index],
            recv_sem=small_recv.at[index],
            device_id=device_id,
            device_id_type=MESH,
        )

    def to_peers(source, target, index):
        for k in range(1, devices):
            peer = lax.rem(me + k, devices)
            small_copy(source, target.at[me], index, {"seq": peer}).start()

    def share_squares(squares):
        sq_send[0] = squares
        sq_recv[mine] = squares
        for k in range(1, groups):
            peer = lax.rem(mine + k, groups)
            small_copy(sq_send.at[0], sq_recv.at[mine], 1, {"ch": peer}).start()

    def share_totals():
        wait_bytes(sq_recv.at[pl.ds(0, groups - 1)], small_recv.at[1])
        total = sq_recv[0]
        for k in range(1, groups):
            total = total + sq_recv[k]
        sq_send[1] = total
        sq_home[me] = total
        to_peers(sq_send.at[1], sq_home, 2)

    first = lax.broadcasted_iota(jnp.int32, (half, LANES), 1) < low

    def pack(source, signal):
        for j in range(blocks):
            even = source[j, pl.ds(0, half, stride=2), :]
            odd = source[j, pl.ds(1, half, stride=2), :]
            send[signal, 2 * j] = jnp.where(first, even, pltpu.roll(odd, low, 1))
            send[signal, 2 * j + 1] = jnp.where(first, pltpu.roll(even, low, 1), odd)

    wait_bytes(gates.at[pl.ds(0, 2)], load_sem.at[0])
    for j in range(blocks):
        x_buf[j] = gate(0, j) * gate(1, j)
    pack(x_buf, 0)
    pl.semaphore_wait(barrier, devices + groups - 2)

    @pl.when(early)
    def _():
        give_far(0, range(split))

    @pl.when(near_here)
    def _():
        give_whole(0)

    @pl.when(whole_here)
    def _():
        give_near(0, 0)
        give_whole(0, True)

    @pl.when(late)
    def _():
        give_whole(0)
        give_far(0, range(side), True)

    wait_bytes(gates.at[pl.ds(2, 2)], load_sem.at[1])
    for j in range(blocks):
        g_buf[j] = gate(2, j) * gate(3, j)
    pack(g_buf, 1)

    @pl.when(near_here)
    def _():
        give_whole(1)

    @pl.when(whole_here)
    def _():
        give_near(1, 0)
        give_whole(1, True)
        for slot in (1, 2):
            for signal in (0, 1):
                give_near(signal, slot)

    @pl.when(late)
    def _():
        give_whole(1)
        give_far(1, range(side), True)
        for signal in (0, 1):
            give_far(signal, range(side, split), True)

    wait_bytes(wide, load_sem.at[2])
    pack(wide, 2)

    @pl.when(near_here)
    def _():
        give_far(2, range(split))
        give_whole(2)
        for signal in range(3):
            for slot in range(3):
                give_near(signal, slot, True)

    @pl.when(whole_here)
    def _():
        give_whole(2, True)
        for slot in range(3):
            give_near(2, slot)

    @pl.when(late)
    def _():
        give_whole(2)
        give_far(2, range(split), True)
        extra[...] = jnp.zeros(extra.shape, jnp.float32)

    part_send[...] = jnp.zeros((8, LANES), jnp.float32)
    for j in range(blocks):
        part_send[pl.ds(j, 1), :] = jnp.sum(x_buf[j] * g_buf[j], axis=0, keepdims=True) * time_scale
    part_home[me] = part_send[...]
    to_peers(part_send, part_home, 0)
    sq_acc[...] = jnp.zeros((8, LANES), jnp.float32)
    for load in loads:
        load.wait()

    def times(which, pieces, at_row, at_column):
        high, rest = pieces
        both = jnp.concatenate([high, rest], axis=1)
        main = jnp.dot(
            table[2 * which, at_row, at_column], both, preferred_element_type=jnp.float32
        )
        small = jnp.dot(
            table[2 * which + 1, at_row, at_column], high, preferred_element_type=jnp.float32
        )
        return main[:, :LANES] + (main[:, LANES:] + small)

    full = slice(0, points)
    early_part = slice(0, points // 2)
    late_part = slice(points // 2, points)

    def forward(slot, signal, part):
        start = (slot * 3 + signal) * devices + part.start // half
        sources = (part.stop - part.start) // half
        data = recv[pl.ds(start, sources)].reshape(sources * half, LANES)
        pieces = split_high_low(data)
        spec[slot, signal, 0] = times(0, pieces, full, part)
        spec[slot, signal, 1] = -times(1, pieces, full, part)

    def inverse(slot, kind, part, scale):
        series = times(0, split_high_low(prod[0]), part, full)
        series = series - times(1, split_high_low(prod[1]), part, full)
        series = series * (scale / points)
        start = part.start // half
        sources = (part.stop - part.start) // half
        back[slot, kind, start : start + sources] = series.reshape(sources, half, LANES)
        return series

    def square_sum(series):
        sq_acc[...] += jnp.sum((series * series).reshape(side * half // 8, 8, LANES), axis=0)

    step = 128

    def halves(slot, ref_row, part, at):
        value = spec[slot, ref_row, part, at, :]
        turned = pltpu.roll(value, low, 1)
        left = lax.broadcasted_iota(jnp.int32, (step, LANES), 1) < low
        return value, turned, jnp.where(left, value, turned), jnp.where(left, turned, value)

    def products(slot, signal, other_signal, conjugate):
        sign = jnp.where(lax.broadcasted_iota(jnp.int32, (step, LANES), 1) < low, 1.0, -1.0)

        @pl.loop(0, points // step)
        def _(index):
            at = pl.ds(pl.multiple_of(index * step, step), step)
            cosine = twist[0, at, :]
            sine = twist[1, at, :]
            signed = sine * sign
            _, _, even_re, odd_re = halves(slot, other_signal, 0, at)
            _, _, even_im, odd_im = halves(slot, other_signal, 1, at)
            a_re, as_re, _, _ = halves(slot, signal, 0, at)
            a_im, as_im, _, _ = halves(slot, signal, 1, at)
            p_re = even_re * cosine - even_im * sine
            p_im = even_im * cosine + even_re * sine
            if conjugate:
                r_re = odd_re * cosine - odd_im * signed
                r_im = odd_im * cosine + odd_re * signed
                prod[0, at, :] = a_re * p_re + a_im * p_im + (as_re * r_re + as_im * r_im)
                prod[1, at, :] = a_im * p_re - a_re * p_im + (as_im * r_re - as_re * r_im)
            else:
                r_re = odd_re * cosine + odd_im * signed
                r_im = odd_im * cosine - odd_re * signed
                prod[0, at, :] = a_re * p_re - a_im * p_im + (as_re * r_re - as_im * r_im)
                prod[1, at, :] = a_im * p_re + a_re * p_im + (as_im * r_re + as_re * r_im)

    @pl.when(near_here)
    def _():
        @pl.loop(0, 3)
        def _(slot):
            c = slot * pair + me
            for signal in (0, 1):
                await_input(slot, signal, 0, side)
                forward(slot, signal, early_part)
            products(slot, 1, 0, True)
            inverse(slot, 0, early_part, time_scale)
            inward(slot, 0, c)

        @pl.loop(0, 3)
        def _(slot):
            c = slot * pair + me
            await_input(slot, 2, 0, side)
            forward(slot, 2, early_part)
            products(slot, 1, 2, True)
            inverse(slot, 1, early_part, 1.0)
            inward(slot, 1, c)
            products(slot, 0, 2, False)
            inverse(slot, 2, early_part, 1.0)
            inward(slot, 2, c)

    def outward(slot, kind, c):
        @pl.when(whole_here)
        def _():
            for k in range(side):
                to_home(slot, kind, c, other + k)

        if kind < 2:
            @pl.when(late)
            def _():
                for k in range(side):
                    to_extra(slot, kind, c, other + k)

        inward(slot, kind, c)

    @pl.when(me >= pair)
    def _():
        zone = me // pair
        slots = 2 - lax.rem(zone, 2)

        @pl.when(late)
        def _():
            await_input(0, 1, side, side)

        @pl.loop(0, slots)
        def _(slot):
            c = lax.rem(me + side + side * slot, devices)

            @pl.when(late & (slot > 0))
            def _():
                await_input(slot, 1, side, side)

            @pl.when(late)
            def _():
                forward(slot, 1, late_part)

            await_input(slot, 0, 0, devices)

            @pl.when(whole_here)
            def _():
                give_far(2, range(split))
                await_input(slot, 1, 0, devices)
                forward(slot, 1, full)

            forward(slot, 0, full)
            products(slot, 1, 0, True)
            series = inverse(slot, 0, full, time_scale)
            outward(slot, 0, c)
            square_sum(series[points // 2 :])

        @pl.when(late)
        def _():
            share_squares(sq_acc[...])

        await_input(0, 2, 0, devices)

        @pl.when(late)
        def _():
            share_totals()

        @pl.loop(0, slots)
        def _(slot):
            c = lax.rem(me + side + side * slot, devices)

            @pl.when(slot > 0)
            def _():
                await_input(slot, 2, 0, devices)

            forward(slot, 2, full)
            products(slot, 1, 2, True)
            inverse(slot, 1, full, 1.0)
            outward(slot, 1, c)
            products(slot, 0, 2, False)
            inverse(slot, 2, full, 1.0)
            outward(slot, 2, c)

    def await_home(kind):
        wait_bytes(home.at[kind], home_recv.at[kind])
        if kind < 2:
            @pl.when(early)
            def _():
                wait_bytes(extra.at[kind], extra_recv.at[kind])

    def unpack(kind, j):
        pieces = []
        for c in (2 * j, 2 * j + 1):
            value = home[kind, c]
            pieces.append(value + extra[kind, c] if kind < 2 and c < split else value)
        left, right = pieces
        flat[j, pl.ds(0, half, stride=2), :] = jnp.where(first, left, pltpu.roll(right, low, 1))
        flat[j, pl.ds(1, half, stride=2), :] = jnp.where(first, pltpu.roll(left, low, 1), right)
        return flat[j]

    wait_bytes(part_home.at[pl.ds(0, devices - 1)], small_recv.at[0])
    direct = part_home[0]
    for k in range(1, devices):
        direct = direct + part_home[k]
    for j in range(blocks):
        dskip_ref[:, columns_of(j)] = direct[j : j + 1]

    await_home(0)
    squares = sq_acc[...] + direct * direct * (1.0 / side)
    for j in range(blocks):
        value = unpack(0, j)
        dh_ref[:, columns_of(j)] = value
        squares = squares + jnp.sum((value * value).reshape(rows // 8, 8, LANES), axis=0)

    @pl.when(early)
    def _():
        share_squares(squares)

    def assemble_inner():
        await_home(2)
        for j in range(blocks):
            at = columns_of(j)
            inner = unpack(2, j) + skip_ref[:, at] * x_buf[j]
            out_ref[:, at] = (gate(2, j) * inner).astype(jnp.bfloat16)
            dq_ref[:, at] = (gate(3, j) * inner).astype(jnp.bfloat16)

    def assemble_grad():
        await_home(1)
        for j in range(blocks):
            at = columns_of(j)
            grad = unpack(1, j) + skip_ref[:, at] * g_buf[j]
            dk_ref[:, at] = (grad * gate(1, j)).astype(jnp.bfloat16)
            dv_ref[:, at] = (grad * gate(0, j)).astype(jnp.bfloat16)

    @pl.when(near_here)
    def _():
        assemble_inner()

    @pl.when(early)
    def _():
        share_totals()

    @pl.when(me >= pair)
    def _():
        assemble_inner()

    assemble_grad()

    wait_bytes(sq_home.at[pl.ds(0, devices - 1)], small_recv.at[2])
    total = sq_home[0]
    for k in range(1, devices):
        total = total + sq_home[k]
    total = jnp.sum(jnp.sum(total, axis=0, keepdims=True), axis=1, keepdims=True)
    rms_ref[...] = jnp.sqrt(total / count)

    for condition, sent, returned in (
        (near_here, 3 * (split - 3) + 2 * split + 3 * pair, 9 * (side - 1)),
        (whole_here, 5 * split + 3 * (pair - 1), 3 * (devices - 1)),
        (far_two, 3 * (split - 2) + 3 * pair, 2 * (2 * side + 3 * (side - 1))),
        (far_one, 3 * (split - 1) + 3 * pair, 2 * side + 3 * (side - 1)),
    ):
        @pl.when(condition)
        def _():
            wait_bytes(recv.at[pl.ds(0, sent)], in_send.at[0])
            wait_bytes(recv.at[pl.ds(0, returned)], out_send.at[0])

    wait_bytes(part_home.at[pl.ds(0, devices - 1)], small_send.at[0])
    wait_bytes(sq_recv.at[pl.ds(0, groups - 1)], small_send.at[1])
    wait_bytes(sq_home.at[pl.ds(0, devices - 1)], small_send.at[2])


def emit(*refs):
    sources, targets, sem = refs[:7], refs[7:14], refs[14]
    copies = [
        pltpu.make_async_copy(source, target, sem.at[index])
        for index, (source, target) in enumerate(zip(sources, targets))
    ]
    for copy in copies:
        copy.start()
    for copy in copies:
        copy.wait()


def fused_body(query_input, key_input, value_input, cotangent, filter_taps, skip_gain):
    devices = lax.axis_size("seq")
    groups = lax.axis_size("ch")
    rows, channels = query_input.shape
    half = rows // 2
    points = half * devices
    tables, twists = half_tables(points)
    count = float(channels * groups * (rows * devices + 1))
    vmem = pl.BlockSpec(memory_space=pltpu.VMEM)
    hbm = pl.BlockSpec(memory_space=pltpu.HBM)
    chunks = 2 * channels // LANES
    blocks = channels // LANES
    shapes = [((rows, channels), jnp.bfloat16)] * 4 + [
        ((rows, channels), jnp.float32),
        ((1, channels), jnp.float32),
        ((1, 1), jnp.float32),
    ]
    held = pl.pallas_call(
        functools.partial(kernel, devices, groups, count),
        out_shape=tuple(pltpu.VMEM(*shape) for shape in shapes),
        in_specs=[hbm] * 8,
        out_specs=(vmem,) * 7,
        scratch_shapes=[
            pltpu.VMEM((4, rows, channels), jnp.bfloat16),
            pltpu.VMEM((1, channels), jnp.float32),
            pltpu.VMEM((blocks, rows, LANES), jnp.float32),
            pltpu.VMEM((blocks, rows, LANES), jnp.float32),
            pltpu.VMEM((blocks, rows, LANES), jnp.float32),
            pltpu.VMEM((blocks, rows, LANES), jnp.float32),
            pltpu.VMEM((3, chunks, half, LANES), jnp.float32),
            pltpu.VMEM((9 * devices, half, LANES), jnp.float32),
            pltpu.VMEM((3, 3, 2, points, LANES), jnp.float32),
            pltpu.VMEM((2, points, LANES), jnp.float32),
            pltpu.VMEM((3, 3, devices, half, LANES), jnp.float32),
            pltpu.VMEM((3, chunks, half, LANES), jnp.float32),
            pltpu.VMEM((2, 3 * (devices // 4), half, LANES), jnp.float32),
            pltpu.VMEM((8, LANES), jnp.float32),
            pltpu.VMEM((devices, 8, LANES), jnp.float32),
            pltpu.VMEM((8, LANES), jnp.float32),
            pltpu.VMEM((2, 8, LANES), jnp.float32),
            pltpu.VMEM((groups, 8, LANES), jnp.float32),
            pltpu.VMEM((devices, 8, LANES), jnp.float32),
            pltpu.VMEM(tables.shape, jnp.bfloat16),
            pltpu.VMEM(twists.shape, jnp.float32),
            pltpu.SemaphoreType.DMA((6,)),
            pltpu.SemaphoreType.DMA((1,)),
            pltpu.SemaphoreType.DMA((9,)),
            pltpu.SemaphoreType.DMA((1,)),
            pltpu.SemaphoreType.DMA((3,)),
            pltpu.SemaphoreType.DMA((2,)),
            pltpu.SemaphoreType.DMA((3,)),
            pltpu.SemaphoreType.DMA((3,)),
        ],
        compiler_params=pltpu.CompilerParams(
            collective_id=0, has_side_effects=True, vmem_limit_bytes=(64 << 20) - (960 << 10)
        ),
    )(
        key_input, value_input, query_input, cotangent, filter_taps,
        skip_gain.reshape(1, channels), jnp.asarray(tables), jnp.asarray(twists),
    )
    results = pl.pallas_call(
        emit,
        out_shape=tuple(jax.ShapeDtypeStruct(*shape) for shape in shapes),
        in_specs=[vmem] * 7,
        out_specs=(hbm,) * 7,
        scratch_shapes=[pltpu.SemaphoreType.DMA((7,))],
        compiler_params=pltpu.CompilerParams(vmem_limit_bytes=4 << 20),
    )(*held)
    return (*results[:5], results[5].reshape(channels), results[6].reshape(()))


def pick_body(query_input, *others):
    devices = lax.axis_size("seq")
    rows, channels = query_input.shape
    fits = devices == 8 and 2 * channels == LANES * devices and rows % 16 == 0
    chosen = fused_body if fits and rows * devices <= 2048 else body
    return chosen(query_input, *others)


def solution(mesh):
    return jax.shard_map(
        pick_body,
        mesh=mesh,
        in_specs=(
            P("seq", "ch"),
            P("seq", "ch"),
            P("seq", "ch"),
            P("seq", "ch"),
            P("seq", "ch"),
            P("ch"),
        ),
        out_specs=(
            P("seq", "ch"),
            P("seq", "ch"),
            P("seq", "ch"),
            P("seq", "ch"),
            P("seq", "ch"),
            P("ch"),
            P(),
        ),
        check_vma=False,
    )
```

time: 46.7 us -> 39.8 us (0.85)
  Pallas kernels: 45.9 us -> 39 us
    pallas_call x1, Pallas kernels: 44.3 us -> 37.5 us  [fused_body(): pl.pallas_call(functools.partial(kernel, devices, groups, count), out_sha...]
where the time goes in v3:
time: 39.8 us; the launch traced here: 39.7 us
  Pallas kernels  39 us (98%)
  between operations  0.64 us (2%)
    pallas_call x1, Pallas kernels, fused_body(): pl.pallas_call(functools.partial(kernel, devices, groups, count), out_sha...  37.5 us
    pallas_call x1, Pallas kernels, fused_body(): pl.pallas_call(emit, out_shape=tuple((jax.ShapeDtypeStruct(*shape) for sh...  1.57 us

profile of v3, /device:TPU:0, one launch (start us, length us, event | category | flops | bytes accessed | tf_op | source)
XLA Modules:
  0.0 39.7 jit_solution(1201835523327901849)
XLA Ops:
  0.6 37.5 %shard_map.135 = (bf16[128,512]{1,0:T(8,128)(2,1)S(1)}, bf16[128,512]{1,0:T(8,128)(2,1)S(1)}, bf16[128,512]{1,0:T(8,128)(2,1)S(1)}, bf16[128,512]{1,0:T(8,128)(2...) custom-call(bf16[128,512]{1,0:T(8,128)(2,1)} %k_hbm.1, bf16[128,512]{1,0:T(8,128)(2,1)} %v_hbm.1, ...), custom_call_target="tpu_custom_call" | custom-call | tf_op jit(solution)/shard_map/pallas_call | solution.py:723
  38.1 1.6 %shard_map.136 = (bf16[128,512]{1,0:T(8,128)(2,1)}, bf16[128,512]{1,0:T(8,128)(2,1)}, bf16[128,512]{1,0:T(8,128)(2,1)}, bf16[128,512]{1,0:T(8,128)(2,1)}, f32[12...) custom-call(bf16[128,512]{1,0:T(8,128)(2,1)S(1)} %get-tuple-element.21.refs_0_, ...), custom_call_target="tpu_custom_call" | custom-call | tf_op jit(solution)/shard_map/pallas_call | solution.py:766

commit v4 on v3

--- a/solution.py
+++ b/solution.py
@@ -186,8 +186,8 @@
     out_ref, dq_ref, dk_ref, dv_ref, dh_ref, dskip_ref, rms_ref,
     gates, skip_ref, x_buf, g_buf, wide, flat,
     send, recv, spec, prod, back, home, extra,
-    part_send, part_home, sq_acc, sq_send, sq_recv, sq_home, table, twist,
-    load_sem, in_send, in_recv, out_send, home_recv, extra_recv, small_send, small_recv,
+    part_send, part_home, sq_acc, sq_send, sq_all, table, twist,
+    load_sem, in_send, in_recv, out_send, home_recv, extra_recv, small_send, small_recv, ready,
 ):
     me = lax.axis_index("seq")
     mine = lax.axis_index("ch")
@@ -210,14 +210,23 @@
     far_one = me >= split
 
     barrier = pltpu.get_barrier_semaphore()
-    for k in range(1, devices):
-        pl.semaphore_signal(
-            barrier, inc=1, device_id={"seq": lax.rem(me + k, devices)}, device_id_type=MESH
-        )
     for k in range(1, groups):
         pl.semaphore_signal(
             barrier, inc=1, device_id={"ch": lax.rem(mine + k, groups)}, device_id_type=MESH
         )
+
+    @pl.when(me < split)
+    def _():
+        for k in range(1, devices):
+            pl.semaphore_signal(
+                barrier, inc=1, device_id={"seq": lax.rem(me + k, devices)}, device_id_type=MESH
+            )
+
+    @pl.when(far_one)
+    def _():
+        for k in range(1, pair):
+            peer = split + lax.rem(me - split + k, pair)
+            pl.semaphore_signal(barrier, inc=1, device_id={"seq": peer}, device_id_type=MESH)
 
     def columns_of(j):
         return pl.ds(j * LANES, LANES)
@@ -233,6 +242,14 @@
     )
     for load in loads:
         load.start()
+
+    @pl.when(far_one)
+    def _():
+        pl.semaphore_wait(barrier, devices + groups - 2)
+        for device in range(split):
+            pl.semaphore_signal(
+                ready, inc=1, device_id={"seq": jnp.int32(device)}, device_id_type=MESH
+            )
 
     def gate(index, j):
         return gates[index, :, columns_of(j)].astype(jnp.float32)
@@ -331,20 +348,14 @@
             small_copy(source, target.at[me], index, {"seq": peer}).start()
 
     def share_squares(squares):
-        sq_send[0] = squares
-        sq_recv[mine] = squares
-        for k in range(1, groups):
-            peer = lax.rem(mine + k, groups)
-            small_copy(sq_send.at[0], sq_recv.at[mine], 1, {"ch": peer}).start()
-
-    def share_totals():
-        wait_bytes(sq_recv.at[pl.ds(0, groups - 1)], small_recv.at[1])
-        total = sq_recv[0]
-        for k in range(1, groups):
-            total = total + sq_recv[k]
-        sq_send[1] = total
-        sq_home[me] = total
-        to_peers(sq_send.at[1], sq_home, 2)
+        row = jnp.sum(squares, axis=0, keepdims=True)
+        sq_send[0] = row
+        sq_all[me * groups + mine] = row
+        for k in range(devices):
+            for n in range(groups):
+                if k or n:
+                    peer = {"seq": lax.rem(me + k, devices), "ch": lax.rem(mine + n, groups)}
+                    small_copy(sq_send.at[0], sq_all.at[me * groups + mine], 1, peer).start()
 
     first = lax.broadcasted_iota(jnp.int32, (half, LANES), 1) < low
 
@@ -359,11 +370,16 @@
     for j in range(blocks):
         x_buf[j] = gate(0, j) * gate(1, j)
     pack(x_buf, 0)
-    pl.semaphore_wait(barrier, devices + groups - 2)
+    @pl.when(me < split)
+    def _():
+        pl.semaphore_wait(barrier, split + groups - 2)
+
+    to_two = (*range(pair), *range(side, split))
+    to_one = range(pair, side)
 
     @pl.when(early)
     def _():
-        give_far(0, range(split))
+        give_far(0, to_two)
 
     @pl.when(near_here)
     def _():
@@ -374,10 +390,14 @@
         give_near(0, 0)
         give_whole(0, True)
 
-    @pl.when(late)
+    @pl.when(far_two)
     def _():
         give_whole(0)
-        give_far(0, range(side), True)
+        give_far(0, range(pair), True)
+
+    @pl.when(far_one)
+    def _():
+        give_far(0, range(pair))
 
     wait_bytes(gates.at[pl.ds(2, 2)], load_sem.at[1])
     for j in range(blocks):
@@ -392,23 +412,46 @@
     def _():
         give_near(1, 0)
         give_whole(1, True)
-        for slot in (1, 2):
-            for signal in (0, 1):
-                give_near(signal, slot)
-
-    @pl.when(late)
+
+    @pl.when(far_two)
     def _():
         give_whole(1)
-        give_far(1, range(side), True)
+        give_far(1, range(pair), True)
         for signal in (0, 1):
             give_far(signal, range(side, split), True)
 
+    @pl.when(far_one)
+    def _():
+        give_far(1, range(pair))
+        give_whole(0)
+        give_whole(1)
+        for signal in (0, 1):
+            give_far(signal, to_one, True)
+        for signal in (0, 1):
+            give_far(signal, range(side, split))
+
     wait_bytes(wide, load_sem.at[2])
     pack(wide, 2)
 
+    @pl.when(whole_here)
+    def _():
+        give_whole(2, True)
+
+    @pl.when(far_two)
+    def _():
+        give_whole(2)
+
+    @pl.when(me < split)
+    def _():
+        pl.semaphore_wait(ready, pair)
+
+    @pl.when(early)
+    def _():
+        give_far(0, to_one)
+
     @pl.when(near_here)
     def _():
-        give_far(2, range(split))
+        give_far(2, (*to_two, *to_one))
         give_whole(2)
         for signal in range(3):
             for slot in range(3):
@@ -416,17 +459,29 @@
 
     @pl.when(whole_here)
     def _():
-        give_whole(2, True)
+        for slot in (1, 2):
+            for signal in (0, 1):
+                give_near(signal, slot)
         for slot in range(3):
             give_near(2, slot)
 
+    @pl.when(far_two)
+    def _():
+        for signal in (0, 1):
+            give_far(signal, to_one)
+        give_far(2, to_two, True)
+        give_far(2, to_one)
+
+    @pl.when(far_one)
+    def _():
+        give_whole(2)
+        give_far(2, to_two)
+        give_far(2, to_one, True)
+
     @pl.when(late)
     def _():
-        give_whole(2)
-        give_far(2, range(split), True)
         extra[...] = jnp.zeros(extra.shape, jnp.float32)
 
-    part_send[...] = jnp.zeros((8, LANES), jnp.float32)
     for j in range(blocks):
         part_send[pl.ds(j, 1), :] = jnp.sum(x_buf[j] * g_buf[j], axis=0, keepdims=True) * time_scale
     part_home[me] = part_send[...]
@@ -565,13 +620,14 @@
 
             await_input(slot, 0, 0, devices)
 
+            forward(slot, 0, full)
+
             @pl.when(whole_here)
             def _():
-                give_far(2, range(split))
                 await_input(slot, 1, 0, devices)
                 forward(slot, 1, full)
-
-            forward(slot, 0, full)
+                give_far(2, (*to_two, *to_one))
+
             products(slot, 1, 0, True)
             series = inverse(slot, 0, full, time_scale)
             outward(slot, 0, c)
@@ -581,20 +637,10 @@
         def _():
             share_squares(sq_acc[...])
 
-        await_input(0, 2, 0, devices)
-
-        @pl.when(late)
-        def _():
-            share_totals()
-
         @pl.loop(0, slots)
         def _(slot):
             c = lax.rem(me + side + side * slot, devices)
-
-            @pl.when(slot > 0)
-            def _():
-                await_input(slot, 2, 0, devices)
-
+            await_input(slot, 2, 0, devices)
             forward(slot, 2, full)
             products(slot, 1, 2, True)
             inverse(slot, 1, full, 1.0)
@@ -628,7 +674,9 @@
         dskip_ref[:, columns_of(j)] = direct[j : j + 1]
 
     await_home(0)
-    squares = sq_acc[...] + direct * direct * (1.0 / side)
+    squares = sq_acc[...]
+    for j in range(blocks):
+        squares = squares + direct[j : j + 1] * direct[j : j + 1] * (1.0 / (8 * side))
     for j in range(blocks):
         value = unpack(0, j)
         dh_ref[:, columns_of(j)] = value
@@ -654,25 +702,15 @@
             dk_ref[:, at] = (grad * gate(1, j)).astype(jnp.bfloat16)
             dv_ref[:, at] = (grad * gate(0, j)).astype(jnp.bfloat16)
 
-    @pl.when(near_here)
-    def _():
-        assemble_inner()
-
-    @pl.when(early)
-    def _():
-        share_totals()
-
-    @pl.when(me >= pair)
-    def _():
-        assemble_inner()
-
+    assemble_inner()
     assemble_grad()
 
-    wait_bytes(sq_home.at[pl.ds(0, devices - 1)], small_recv.at[2])
-    total = sq_home[0]
-    for k in range(1, devices):
-        total = total + sq_home[k]
-    total = jnp.sum(jnp.sum(total, axis=0, keepdims=True), axis=1, keepdims=True)
+    everyone = devices * groups
+    wait_bytes(sq_all.at[pl.ds(0, everyone - 1)], small_recv.at[1])
+    total = sq_all[0]
+    for k in range(1, everyone):
+        total = total + sq_all[k]
+    total = jnp.sum(total, axis=1, keepdims=True)
     rms_ref[...] = jnp.sqrt(total / count)
 
     for condition, sent, returned in (
@@ -687,8 +725,7 @@
             wait_bytes(recv.at[pl.ds(0, returned)], out_send.at[0])
 
     wait_bytes(part_home.at[pl.ds(0, devices - 1)], small_send.at[0])
-    wait_bytes(sq_recv.at[pl.ds(0, groups - 1)], small_send.at[1])
-    wait_bytes(sq_home.at[pl.ds(0, devices - 1)], small_send.at[2])
+    wait_bytes(sq_all.at[pl.ds(0, everyone - 1)], small_send.at[1])
 
 
 def emit(*refs):
@@ -739,12 +776,11 @@
             pltpu.VMEM((3, 3, devices, half, LANES), jnp.float32),
             pltpu.VMEM((3, chunks, half, LANES), jnp.float32),
             pltpu.VMEM((2, 3 * (devices // 4), half, LANES), jnp.float32),
+            pltpu.VMEM((blocks, LANES), jnp.float32),
+            pltpu.VMEM((devices, blocks, LANES), jnp.float32),
             pltpu.VMEM((8, LANES), jnp.float32),
-            pltpu.VMEM((devices, 8, LANES), jnp.float32),
-            pltpu.VMEM((8, LANES), jnp.float32),
-            pltpu.VMEM((2, 8, LANES), jnp.float32),
-            pltpu.VMEM((groups, 8, LANES), jnp.float32),
-            pltpu.VMEM((devices, 8, LANES), jnp.float32),
+            pltpu.VMEM((1, 1, LANES), jnp.float32),
+            pltpu.VMEM((devices * groups, 1, LANES), jnp.float32),
             pltpu.VMEM(tables.shape, jnp.bfloat16),
             pltpu.VMEM(twists.shape, jnp.float32),
             pltpu.SemaphoreType.DMA((6,)),
@@ -753,8 +789,9 @@
             pltpu.SemaphoreType.DMA((1,)),
             pltpu.SemaphoreType.DMA((3,)),
             pltpu.SemaphoreType.DMA((2,)),
-            pltpu.SemaphoreType.DMA((3,)),
-            pltpu.SemaphoreType.DMA((3,)),
+            pltpu.SemaphoreType.DMA((2,)),
+            pltpu.SemaphoreType.DMA((2,)),
+            pltpu.SemaphoreType.REGULAR,
         ],
         compiler_params=pltpu.CompilerParams(
             collective_id=0, has_side_effects=True, vmem_limit_bytes=(64 << 20) - (960 << 10)

time: 39.8 us -> 37.5 us (0.942)
  Pallas kernels: 39 us -> 36.7 us
    pallas_call x1, Pallas kernels: 37.5 us -> 35.1 us  [fused_body(): pl.pallas_call(functools.partial(kernel, devices, groups, count), out_sha...]
where the time goes in v4:
time: 37.5 us; the launch traced here: 37.3 us
  Pallas kernels  36.7 us (98%)
  between operations  0.64 us (2%)
    pallas_call x1, Pallas kernels, fused_body(): pl.pallas_call(functools.partial(kernel, devices, groups, count), out_sha...  35.1 us
    pallas_call x1, Pallas kernels, fused_body(): pl.pallas_call(emit, out_shape=tuple((jax.ShapeDtypeStruct(*shape) for sh...  1.57 us

profile of v4, /device:TPU:0, one launch (start us, length us, event | category | flops | bytes accessed | tf_op | source)
XLA Modules:
  0.0 37.3 jit_solution(7416063808491200385)
XLA Ops:
  0.6 35.1 %shard_map.135 = (bf16[128,512]{1,0:T(8,128)(2,1)S(1)}, bf16[128,512]{1,0:T(8,128)(2,1)S(1)}, bf16[128,512]{1,0:T(8,128)(2,1)S(1)}, bf16[128,512]{1,0:T(8,128)(2...) custom-call(bf16[128,512]{1,0:T(8,128)(2,1)} %k_hbm.1, bf16[128,512]{1,0:T(8,128)(2,1)} %v_hbm.1, ...), custom_call_target="tpu_custom_call" | custom-call | tf_op jit(solution)/shard_map/pallas_call | solution.py:760
  35.8 1.6 %shard_map.136 = (bf16[128,512]{1,0:T(8,128)(2,1)}, bf16[128,512]{1,0:T(8,128)(2,1)}, bf16[128,512]{1,0:T(8,128)(2,1)}, bf16[128,512]{1,0:T(8,128)(2,1)}, f32[12...) custom-call(bf16[128,512]{1,0:T(8,128)(2,1)S(1)} %get-tuple-element.21.refs_0_, ...), custom_call_target="tpu_custom_call" | custom-call | tf_op jit(solution)/shard_map/pallas_call | solution.py:803

commit v5 on v4

--- a/solution.py
+++ b/solution.py
@@ -186,7 +186,7 @@
     out_ref, dq_ref, dk_ref, dv_ref, dh_ref, dskip_ref, rms_ref,
     gates, skip_ref, x_buf, g_buf, wide, flat,
     send, recv, spec, prod, back, home, extra,
-    part_send, part_home, sq_acc, sq_send, sq_all, table, twist,
+    part_send, part_home, half_send, half_home, sq_acc, sq_send, sq_all, table, twist,
     load_sem, in_send, in_recv, out_send, home_recv, extra_recv, small_send, small_recv, ready,
 ):
     me = lax.axis_index("seq")
@@ -342,10 +342,14 @@
             device_id_type=MESH,
         )
 
-    def to_peers(source, target, index):
-        for k in range(1, devices):
-            peer = lax.rem(me + k, devices)
-            small_copy(source, target.at[me], index, {"seq": peer}).start()
+    def share_part():
+        wait_bytes(part_home.at[pl.ds(0, side - 1)], small_recv.at[0])
+        part = part_home[base]
+        for k in range(1, side):
+            part = part + part_home[base + k]
+        half_send[...] = part
+        peer = lax.rem(me + side, devices)
+        small_copy(half_send, half_home, 2, {"seq": peer}).start()
 
     def share_squares(squares):
         row = jnp.sum(squares, axis=0, keepdims=True)
@@ -384,6 +388,8 @@
     @pl.when(near_here)
     def _():
         give_whole(0)
+        for slot in range(3):
+            give_near(0, slot, True)
 
     @pl.when(whole_here)
     def _():
@@ -407,6 +413,8 @@
     @pl.when(near_here)
     def _():
         give_whole(1)
+        for slot in range(3):
+            give_near(1, slot, True)
 
     @pl.when(whole_here)
     def _():
@@ -453,9 +461,8 @@
     def _():
         give_far(2, (*to_two, *to_one))
         give_whole(2)
-        for signal in range(3):
-            for slot in range(3):
-                give_near(signal, slot, True)
+        for slot in range(3):
+            give_near(2, slot, True)
 
     @pl.when(whole_here)
     def _():
@@ -485,7 +492,9 @@
     for j in range(blocks):
         part_send[pl.ds(j, 1), :] = jnp.sum(x_buf[j] * g_buf[j], axis=0, keepdims=True) * time_scale
     part_home[me] = part_send[...]
-    to_peers(part_send, part_home, 0)
+    for k in range(1, side):
+        peer = base + lax.rem(me - base + k, side)
+        small_copy(part_send, part_home.at[me], 0, {"seq": peer}).start()
     sq_acc[...] = jnp.zeros((8, LANES), jnp.float32)
     for load in loads:
         load.wait()
@@ -635,6 +644,7 @@
 
         @pl.when(late)
         def _():
+            share_part()
             share_squares(sq_acc[...])
 
         @pl.loop(0, slots)
@@ -645,6 +655,10 @@
             products(slot, 1, 2, True)
             inverse(slot, 1, full, 1.0)
             outward(slot, 1, c)
+
+        @pl.loop(0, slots)
+        def _(slot):
+            c = lax.rem(me + side + side * slot, devices)
             products(slot, 0, 2, False)
             inverse(slot, 2, full, 1.0)
             outward(slot, 2, c)
@@ -666,10 +680,9 @@
         flat[j, pl.ds(1, half, stride=2), :] = jnp.where(first, pltpu.roll(left, low, 1), right)
         return flat[j]
 
-    wait_bytes(part_home.at[pl.ds(0, devices - 1)], small_recv.at[0])
-    direct = part_home[0]
-    for k in range(1, devices):
-        direct = direct + part_home[k]
+    pl.when(early)(share_part)
+    wait_bytes(half_home, small_recv.at[2])
+    direct = half_send[...] + half_home[...]
     for j in range(blocks):
         dskip_ref[:, columns_of(j)] = direct[j : j + 1]
 
@@ -702,16 +715,20 @@
             dk_ref[:, at] = (grad * gate(1, j)).astype(jnp.bfloat16)
             dv_ref[:, at] = (grad * gate(0, j)).astype(jnp.bfloat16)
 
+    everyone = devices * groups
+
+    def finish_squares():
+        wait_bytes(sq_all.at[pl.ds(0, everyone - 1)], small_recv.at[1])
+        total = sq_all[0]
+        for k in range(1, everyone):
+            total = total + sq_all[k]
+        total = jnp.sum(total, axis=1, keepdims=True)
+        rms_ref[...] = jnp.sqrt(total / count)
+
     assemble_inner()
+    pl.when(early)(finish_squares)
     assemble_grad()
-
-    everyone = devices * groups
-    wait_bytes(sq_all.at[pl.ds(0, everyone - 1)], small_recv.at[1])
-    total = sq_all[0]
-    for k in range(1, everyone):
-        total = total + sq_all[k]
-    total = jnp.sum(total, axis=1, keepdims=True)
-    rms_ref[...] = jnp.sqrt(total / count)
+    pl.when(late)(finish_squares)
 
     for condition, sent, returned in (
         (near_here, 3 * (split - 3) + 2 * split + 3 * pair, 9 * (side - 1)),
@@ -724,7 +741,8 @@
             wait_bytes(recv.at[pl.ds(0, sent)], in_send.at[0])
             wait_bytes(recv.at[pl.ds(0, returned)], out_send.at[0])
 
-    wait_bytes(part_home.at[pl.ds(0, devices - 1)], small_send.at[0])
+    wait_bytes(part_home.at[pl.ds(0, side - 1)], small_send.at[0])
+    wait_bytes(half_home, small_send.at[2])
     wait_bytes(sq_all.at[pl.ds(0, everyone - 1)], small_send.at[1])
 
 
@@ -778,6 +796,8 @@
             pltpu.VMEM((2, 3 * (devices // 4), half, LANES), jnp.float32),
             pltpu.VMEM((blocks, LANES), jnp.float32),
             pltpu.VMEM((devices, blocks, LANES), jnp.float32),
+            pltpu.VMEM((blocks, LANES), jnp.float32),
+            pltpu.VMEM((blocks, LANES), jnp.float32),
             pltpu.VMEM((8, LANES), jnp.float32),
             pltpu.VMEM((1, 1, LANES), jnp.float32),
             pltpu.VMEM((devices * groups, 1, LANES), jnp.float32),
@@ -789,8 +809,8 @@
             pltpu.SemaphoreType.DMA((1,)),
             pltpu.SemaphoreType.DMA((3,)),
             pltpu.SemaphoreType.DMA((2,)),
-            pltpu.SemaphoreType.DMA((2,)),
-            pltpu.SemaphoreType.DMA((2,)),
+            pltpu.SemaphoreType.DMA((3,)),
+            pltpu.SemaphoreType.DMA((3,)),
             pltpu.SemaphoreType.REGULAR,
         ],
         compiler_params=pltpu.CompilerParams(

time: 37.5 us -> 36.8 us (0.981)
  Pallas kernels: 36.7 us -> 36 us
    pallas_call x1, Pallas kernels: 35.1 us -> 34.4 us  [fused_body(): pl.pallas_call(functools.partial(kernel, devices, groups, count), out_sha...]
where the time goes in v5:
time: 36.8 us; the launch traced here: 36.6 us
  Pallas kernels  36 us (98%)
  between operations  0.64 us (2%)
    pallas_call x1, Pallas kernels, fused_body(): pl.pallas_call(functools.partial(kernel, devices, groups, count), out_sha...  34.4 us
    pallas_call x1, Pallas kernels, fused_body(): pl.pallas_call(emit, out_shape=tuple((jax.ShapeDtypeStruct(*shape) for sh...  1.57 us

profile of v5, /device:TPU:0, one launch (start us, length us, event | category | flops | bytes accessed | tf_op | source)
XLA Modules:
  0.0 36.6 jit_solution(4638469062297079664)
XLA Ops:
  0.6 34.4 %shard_map.135 = (bf16[128,512]{1,0:T(8,128)(2,1)S(1)}, bf16[128,512]{1,0:T(8,128)(2,1)S(1)}, bf16[128,512]{1,0:T(8,128)(2,1)S(1)}, bf16[128,512]{1,0:T(8,128)(2...) custom-call(bf16[128,512]{1,0:T(8,128)(2,1)} %k_hbm.1, bf16[128,512]{1,0:T(8,128)(2,1)} %v_hbm.1, ...), custom_call_target="tpu_custom_call" | custom-call | tf_op jit(solution)/shard_map/pallas_call | solution.py:778
  35.1 1.6 %shard_map.136 = (bf16[128,512]{1,0:T(8,128)(2,1)}, bf16[128,512]{1,0:T(8,128)(2,1)}, bf16[128,512]{1,0:T(8,128)(2,1)}, bf16[128,512]{1,0:T(8,128)(2,1)}, f32[12...) custom-call(bf16[128,512]{1,0:T(8,128)(2,1)S(1)} %get-tuple-element.21.refs_0_, ...), custom_call_target="tpu_custom_call" | custom-call | tf_op jit(solution)/shard_map/pallas_call | solution.py:823

commit v6 on v5

--- a/solution.py
+++ b/solution.py
@@ -183,7 +183,7 @@
 def kernel(
     devices, groups, count,
     k_hbm, v_hbm, q_hbm, c_hbm, h_hbm, skip_hbm, table_hbm, twist_hbm,
-    out_ref, dq_ref, dk_ref, dv_ref, dh_ref, dskip_ref, rms_ref,
+    out_ref, dq_ref, dk_ref, dv_ref, dh_ref, last_ref,
     gates, skip_ref, x_buf, g_buf, wide, flat,
     send, recv, spec, prod, back, home, extra,
     part_send, part_home, half_send, half_home, sq_acc, sq_send, sq_all, table, twist,
@@ -684,7 +684,7 @@
     wait_bytes(half_home, small_recv.at[2])
     direct = half_send[...] + half_home[...]
     for j in range(blocks):
-        dskip_ref[:, columns_of(j)] = direct[j : j + 1]
+        last_ref[0:1, columns_of(j)] = direct[j : j + 1]
 
     await_home(0)
     squares = sq_acc[...]
@@ -723,7 +723,7 @@
         for k in range(1, everyone):
             total = total + sq_all[k]
         total = jnp.sum(total, axis=1, keepdims=True)
-        rms_ref[...] = jnp.sqrt(total / count)
+        last_ref[1:2, :] = jnp.broadcast_to(jnp.sqrt(total / count), (1, channels))
 
     assemble_inner()
     pl.when(early)(finish_squares)
@@ -747,12 +747,18 @@
 
 
 def emit(*refs):
-    sources, targets, sem = refs[:7], refs[7:14], refs[14]
+    sources, last_ref, targets = refs[:5], refs[5], refs[6:13]
+    skip_row, rms_value, sem = refs[13:]
+    sources = (*sources, skip_row, rms_value)
     copies = [
         pltpu.make_async_copy(source, target, sem.at[index])
         for index, (source, target) in enumerate(zip(sources, targets))
     ]
-    for copy in copies:
+    for copy in copies[:5]:
+        copy.start()
+    skip_row[...] = last_ref[0:1, :]
+    rms_value[...] = last_ref[1:2, 0:1]
+    for copy in copies[5:]:
         copy.start()
     for copy in copies:
         copy.wait()
@@ -777,9 +783,11 @@
     ]
     held = pl.pallas_call(
         functools.partial(kernel, devices, groups, count),
-        out_shape=tuple(pltpu.VMEM(*shape) for shape in shapes),
+        out_shape=tuple(
+            pltpu.VMEM(*shape) for shape in (*shapes[:5], ((2, channels), jnp.float32))
+        ),
         in_specs=[hbm] * 8,
-        out_specs=(vmem,) * 7,
+        out_specs=(vmem,) * 6,
         scratch_shapes=[
             pltpu.VMEM((4, rows, channels), jnp.bfloat16),
             pltpu.VMEM((1, channels), jnp.float32),
@@ -823,9 +831,13 @@
     results = pl.pallas_call(
         emit,
         out_shape=tuple(jax.ShapeDtypeStruct(*shape) for shape in shapes),
-        in_specs=[vmem] * 7,
+        in_specs=[vmem] * 6,
         out_specs=(hbm,) * 7,
-        scratch_shapes=[pltpu.SemaphoreType.DMA((7,))],
+        scratch_shapes=[
+            pltpu.VMEM((1, channels), jnp.float32),
+            pltpu.VMEM((1, 1), jnp.float32),
+            pltpu.SemaphoreType.DMA((7,)),
+        ],
         compiler_params=pltpu.CompilerParams(vmem_limit_bytes=4 << 20),
     )(*held)
     return (*results[:5], results[5].reshape(channels), results[6].reshape(()))

time: 36.8 us -> 35.6 us (0.967)
  Pallas kernels: 36 us -> 34.8 us
    pallas_call x1, Pallas kernels: 1.57 us -> 0.94 us  [fused_body(): pl.pallas_call(emit, out_shape=tuple((jax.ShapeDtypeStruct(*shape) for sh...]
    pallas_call x1, Pallas kernels: 34.4 us -> 33.9 us  [fused_body(): pl.pallas_call(functools.partial(kernel, devices, groups, count), out_sha...]
where the time goes in v6:
time: 35.6 us; the launch traced here: 35.5 us
  Pallas kernels  34.8 us (98%)
  between operations  0.64 us (2%)
    pallas_call x1, Pallas kernels, fused_body(): pl.pallas_call(functools.partial(kernel, devices, groups, count), out_sha...  33.9 us
    pallas_call x1, Pallas kernels, fused_body(): pl.pallas_call(emit, out_shape=tuple((jax.ShapeDtypeStruct(*shape) for sh...  0.94 us

profile of v6, /device:TPU:0, one launch (start us, length us, event | category | flops | bytes accessed | tf_op | source)
XLA Modules:
  0.0 35.5 jit_solution(12969212146853908126)
XLA Ops:
  0.6 33.9 %shard_map.135 = (bf16[128,512]{1,0:T(8,128)(2,1)S(1)}, bf16[128,512]{1,0:T(8,128)(2,1)S(1)}, bf16[128,512]{1,0:T(8,128)(2,1)S(1)}, bf16[128,512]{1,0:T(8,128)(2...) custom-call(bf16[128,512]{1,0:T(8,128)(2,1)} %k_hbm.1, bf16[128,512]{1,0:T(8,128)(2,1)} %v_hbm.1, ...), custom_call_target="tpu_custom_call" | custom-call | tf_op jit(solution)/shard_map/pallas_call | solution.py:784
  34.5 0.9 %shard_map.136 = (bf16[128,512]{1,0:T(8,128)(2,1)}, bf16[128,512]{1,0:T(8,128)(2,1)}, bf16[128,512]{1,0:T(8,128)(2,1)}, bf16[128,512]{1,0:T(8,128)(2,1)}, f32[12...) custom-call(bf16[128,512]{1,0:T(8,128)(2,1)S(1)} %get-tuple-element.20.refs_0_, ...), custom_call_target="tpu_custom_call" | custom-call | tf_op jit(solution)/shard_map/pallas_call | solution.py:831

commit v7 on v6

--- a/solution.py
+++ b/solution.py
@@ -459,7 +459,7 @@
 
     @pl.when(near_here)
     def _():
-        give_far(2, (*to_two, *to_one))
+        give_far(2, range(split))
         give_whole(2)
         for slot in range(3):
             give_near(2, slot, True)
@@ -476,14 +476,12 @@
     def _():
         for signal in (0, 1):
             give_far(signal, to_one)
-        give_far(2, to_two, True)
-        give_far(2, to_one)
+        give_far(2, range(split), True)
 
     @pl.when(far_one)
     def _():
         give_whole(2)
-        give_far(2, to_two)
-        give_far(2, to_one, True)
+        give_far(2, range(split), True)
 
     @pl.when(late)
     def _():
@@ -601,7 +599,7 @@
         if kind < 2:
             @pl.when(late)
             def _():
-                for k in range(side):
+                for k in range(side if kind == 0 else 1):
                     to_extra(slot, kind, c, other + k)
 
         inward(slot, kind, c)
@@ -635,7 +633,7 @@
             def _():
                 await_input(slot, 1, 0, devices)
                 forward(slot, 1, full)
-                give_far(2, (*to_two, *to_one))
+                give_far(2, range(split))
 
             products(slot, 1, 0, True)
             series = inverse(slot, 0, full, time_scale)
@@ -655,6 +653,14 @@
             products(slot, 1, 2, True)
             inverse(slot, 1, full, 1.0)
             outward(slot, 1, c)
+
+        @pl.when(late)
+        def _():
+            @pl.loop(0, slots)
+            def _(slot):
+                c = lax.rem(me + side + side * slot, devices)
+                for k in range(1, side):
+                    to_extra(slot, 1, c, other + k)
 
         @pl.loop(0, slots)
         def _(slot):

time: 35.6 us -> 34.7 us (0.975); the launches traced: 35.5 us -> 34.1 us
  Pallas kernels: 34.8 us -> 33.5 us
    pallas_call x1, Pallas kernels: 33.9 us -> 32.5 us  [fused_body(): pl.pallas_call(functools.partial(kernel, devices, groups, count), out_sha...]
where the time goes in v7:
time: 34.7 us; the launch traced here: 34.1 us
  Pallas kernels  33.5 us (97%)
  between operations  0.64 us (2%)
    pallas_call x1, Pallas kernels, fused_body(): pl.pallas_call(functools.partial(kernel, devices, groups, count), out_sha...  32.5 us
    pallas_call x1, Pallas kernels, fused_body(): pl.pallas_call(emit, out_shape=tuple((jax.ShapeDtypeStruct(*shape) for sh...  0.94 us

profile of v7, /device:TPU:0, one launch (start us, length us, event | category | flops | bytes accessed | tf_op | source)
XLA Modules:
  0.0 34.1 jit_solution(4061900812237265433)
XLA Ops:
  0.6 32.5 %shard_map.135 = (bf16[128,512]{1,0:T(8,128)(2,1)S(1)}, bf16[128,512]{1,0:T(8,128)(2,1)S(1)}, bf16[128,512]{1,0:T(8,128)(2,1)S(1)}, bf16[128,512]{1,0:T(8,128)(2...) custom-call(bf16[128,512]{1,0:T(8,128)(2,1)} %k_hbm.1, bf16[128,512]{1,0:T(8,128)(2,1)} %v_hbm.1, ...), custom_call_target="tpu_custom_call" | custom-call | tf_op jit(solution)/shard_map/pallas_call | solution.py:790
  33.2 0.9 %shard_map.136 = (bf16[128,512]{1,0:T(8,128)(2,1)}, bf16[128,512]{1,0:T(8,128)(2,1)}, bf16[128,512]{1,0:T(8,128)(2,1)}, bf16[128,512]{1,0:T(8,128)(2,1)}, f32[12...) custom-call(bf16[128,512]{1,0:T(8,128)(2,1)S(1)} %get-tuple-element.20.refs_0_, ...), custom_call_target="tpu_custom_call" | custom-call | tf_op jit(solution)/shard_map/pallas_call | solution.py:837

commit v8 on v7

--- a/solution.py
+++ b/solution.py
@@ -591,11 +591,6 @@
             inward(slot, 2, c)
 
     def outward(slot, kind, c):
-        @pl.when(whole_here)
-        def _():
-            for k in range(side):
-                to_home(slot, kind, c, other + k)
-
         if kind < 2:
             @pl.when(late)
             def _():
@@ -603,6 +598,11 @@
                     to_extra(slot, kind, c, other + k)
 
         inward(slot, kind, c)
+
+        @pl.when(whole_here)
+        def _():
+            for k in range(side):
+                to_home(slot, kind, c, other + k)
 
     @pl.when(me >= pair)
     def _():

time: 34.7 us -> 34.7 us (level)
  no operation moved by 1% of the time
where the time goes in v8:
time: 34.7 us; the launch traced here: 34.1 us
  Pallas kernels  33.5 us (97%)
  between operations  0.64 us (2%)
    pallas_call x1, Pallas kernels, fused_body(): pl.pallas_call(functools.partial(kernel, devices, groups, count), out_sha...  32.5 us
    pallas_call x1, Pallas kernels, fused_body(): pl.pallas_call(emit, out_shape=tuple((jax.ShapeDtypeStruct(*shape) for sh...  0.94 us

profile of v8, /device:TPU:0, one launch (start us, length us, event | category | flops | bytes accessed | tf_op | source)
XLA Modules:
  0.0 34.1 jit_solution(2853281716231369551)
XLA Ops:
  0.6 32.5 %shard_map.135 = (bf16[128,512]{1,0:T(8,128)(2,1)S(1)}, bf16[128,512]{1,0:T(8,128)(2,1)S(1)}, bf16[128,512]{1,0:T(8,128)(2,1)S(1)}, bf16[128,512]{1,0:T(8,128)(2...) custom-call(bf16[128,512]{1,0:T(8,128)(2,1)} %k_hbm.1, bf16[128,512]{1,0:T(8,128)(2,1)} %v_hbm.1, ...), custom_call_target="tpu_custom_call" | custom-call | tf_op jit(solution)/shard_map/pallas_call | solution.py:790
  33.2 0.9 %shard_map.136 = (bf16[128,512]{1,0:T(8,128)(2,1)}, bf16[128,512]{1,0:T(8,128)(2,1)}, bf16[128,512]{1,0:T(8,128)(2,1)}, bf16[128,512]{1,0:T(8,128)(2,1)}, f32[12...) custom-call(bf16[128,512]{1,0:T(8,128)(2,1)S(1)} %get-tuple-element.20.refs_0_, ...), custom_call_target="tpu_custom_call" | custom-call | tf_op jit(solution)/shard_map/pallas_call | solution.py:837

commit v9 on v7

--- a/solution.py
+++ b/solution.py
@@ -420,6 +420,9 @@
     def _():
         give_near(1, 0)
         give_whole(1, True)
+        for slot in (1, 2):
+            for signal in (0, 1):
+                give_near(signal, slot)
 
     @pl.when(far_two)
     def _():
@@ -466,9 +469,6 @@
 
     @pl.when(whole_here)
     def _():
-        for slot in (1, 2):
-            for signal in (0, 1):
-                give_near(signal, slot)
         for slot in range(3):
             give_near(2, slot)
 

time: 34.7 us -> 34.7 us (level)
  no operation moved by 1% of the time
where the time goes in v9:
time: 34.7 us; the launch traced here: 34.2 us
  Pallas kernels  33.6 us (97%)
  between operations  0.64 us (2%)
    pallas_call x1, Pallas kernels, fused_body(): pl.pallas_call(functools.partial(kernel, devices, groups, count), out_sha...  32.6 us
    pallas_call x1, Pallas kernels, fused_body(): pl.pallas_call(emit, out_shape=tuple((jax.ShapeDtypeStruct(*shape) for sh...  0.94 us

profile of v9, /device:TPU:0, one launch (start us, length us, event | category | flops | bytes accessed | tf_op | source)
XLA Modules:
  0.0 34.2 jit_solution(12044503758360765967)
XLA Ops:
  0.6 32.6 %shard_map.135 = (bf16[128,512]{1,0:T(8,128)(2,1)S(1)}, bf16[128,512]{1,0:T(8,128)(2,1)S(1)}, bf16[128,512]{1,0:T(8,128)(2,1)S(1)}, bf16[128,512]{1,0:T(8,128)(2...) custom-call(bf16[128,512]{1,0:T(8,128)(2,1)} %k_hbm.1, bf16[128,512]{1,0:T(8,128)(2,1)} %v_hbm.1, ...), custom_call_target="tpu_custom_call" | custom-call | tf_op jit(solution)/shard_map/pallas_call | solution.py:790
  33.3 0.9 %shard_map.136 = (bf16[128,512]{1,0:T(8,128)(2,1)}, bf16[128,512]{1,0:T(8,128)(2,1)}, bf16[128,512]{1,0:T(8,128)(2,1)}, bf16[128,512]{1,0:T(8,128)(2,1)}, f32[12...) custom-call(bf16[128,512]{1,0:T(8,128)(2,1)S(1)} %get-tuple-element.20.refs_0_, ...), custom_call_target="tpu_custom_call" | custom-call | tf_op jit(solution)/shard_map/pallas_call | solution.py:837
